TPU v7x, 512 devices: a whole 4x8x8 slice. The times are simulated.
512 devices in a mesh: inp: 32 (over z, x), tm: 16 (over y, core).
Axes of the slice: x: 4, y: 8, z: 8, core: 2. Of those that a mesh axis runs over, the one named last changes fastest.
Arguments:
- samples: bfloat16 [576, 2, 98304], P('inp', None, 'tm'), may hold values from -6 to 6
- delays: int32 [576], P('inp'), may hold values from 0 to 3840
- taps: int32 [16, 256], replicated, may hold values from -2048 to 2047
Outputs:
- visibilities: float32 [256, 576, 1152], P('inp', 'tm')
All inputs are finite; a program needn't handle non-finite values.
Results may differ from a plain program's by a relative error of at most 0.0031.
Values may be sent and summed in bfloat16 or wider, within the bound.
No kernel may reach another device: no remote copies, remote signals or barrier semaphores. Data moves between devices by JAX's collectives and lax.ppermute only.
A program may use at most 128 MiB of HBM per device.

v0:
```python
import math

import jax
import jax.numpy as jnp
from jax import lax
from jax.sharding import PartitionSpec as P


def shifted(value, axis, by):
    peers = lax.axis_size(axis)
    return lax.ppermute(value, axis, [(i, (i + by) % peers) for i in range(peers)])


def dft_table(length):
    channel_index = jnp.arange(length, dtype=jnp.int32)
    phase = (jnp.outer(channel_index, channel_index) % length).astype(jnp.float32) * (
        2.0 * math.pi / length
    )
    cosine = jnp.cos(phase)
    sine = jnp.sin(phase)
    upper = jnp.concatenate([cosine, -sine], axis=1)
    lower = jnp.concatenate([sine, cosine], axis=1)
    return jnp.concatenate([upper, lower], axis=0) / math.sqrt(length)


def shards(samples, delays, taps):
    tap_count, channels = taps.shape
    local_inputs, _, shard_len = samples.shape
    margin = (tap_count - 1) * channels
    local_spectra = shard_len // channels
    earlier = shifted(samples, "tm", 1)
    later = shifted(samples, "tm", -1)
    padded = jnp.concatenate(
        [earlier[:, :, shard_len - margin :], samples, later[:, :, :margin]], axis=2
    )
    window = shard_len + margin

    def align(series, offset):
        return lax.dynamic_slice_in_dim(series, offset, window, 1)

    aligned = jax.vmap(align)(padded, delays).astype(jnp.float32)
    frames = aligned.reshape(local_inputs, 2, local_spectra + tap_count - 1, channels)
    coefficient = taps.astype(jnp.float32) * (1.0 / 4096.0)
    filtered = jnp.zeros((local_inputs, 2, local_spectra, channels), jnp.float32)
    for tap in range(tap_count):
        begin = tap_count - 1 - tap
        filtered = (
            filtered
            + coefficient[tap][None, None, None, :] * frames[:, :, begin : begin + local_spectra, :]
        )
    table = dft_table(channels).reshape(2, channels, 2, channels)
    spectra = jnp.einsum(
        "icsk,ckdf->fids", filtered, table, precision=lax.Precision.HIGHEST
    ).astype(jnp.bfloat16)
    turned = lax.all_to_all(spectra, "inp", split_axis=0, concat_axis=1, tiled=True)
    local_channels, all_inputs = (turned.shape[0], turned.shape[1])
    time_shards = lax.axis_size("tm")
    rows_count = all_inputs // time_shards
    total_spectra = local_spectra * time_shards
    first_row = lax.axis_index("tm") * rows_count
    piece = lax.all_gather(turned, "tm", axis=3, tiled=True)
    width = piece.shape[3]
    all_rows = piece.reshape(local_channels, all_inputs, 2 * width)
    my_rows = lax.dynamic_slice_in_dim(piece, first_row, rows_count, 1)
    row_block = my_rows.reshape(local_channels, rows_count, 2 * width)
    swapped = jnp.concatenate([my_rows[:, :, 1, :], -my_rows[:, :, 0, :]], axis=2)
    gram_real = jnp.einsum("fas,fbs->fab", row_block, all_rows, preferred_element_type=jnp.float32)
    gram_imag = jnp.einsum("fas,fbs->fab", swapped, all_rows, preferred_element_type=jnp.float32)
    gram_real, gram_imag = (gram_real, gram_imag)
    result = jnp.concatenate([gram_real, gram_imag], axis=2) * (1.0 / total_spectra)
    return result


def solution(mesh):
    in_specs = (P("inp", None, "tm"), P("inp"), P())
    out_specs = P("inp", "tm", None)
    return jax.shard_map(shards, mesh=mesh, in_specs=in_specs, out_specs=out_specs, check_vma=False)
```

profile of v0, /device:TPU:1, one launch (start us, length us, event | category | flops | bytes accessed | tf_op | source)
XLA Modules:
  0.0 221.5 jit_solution(11996081832337151029)
XLA Ops:
  6.5 2.7 %collective-permute-start = (bf16[18,2,6144]{2,1,0:T(2,128)(2,1)}, bf16[18,2,6144]{2,1,0:T(2,128)(2,1)}, u32[]{:S(2)}, u32[]{:S(2)}) collective-permute-start(bf16[18,2,6144]{2,1,0:T(2,128)(2,1)} %param.3), channel_id=1, source_target_pairs={{0,1},{1,2},{2,3},{3,4},{4,5},{5,6},{6,7},{7,8},{8,9},{9,10},{10,1... | collective-permute-start | bytes 1327112 | tf_op jit(solution)/shard_map/ppermute | solution.py:11
  9.2 4.2 %collective-permute-start.1 = (bf16[18,2,6144]{2,1,0:T(2,128)(2,1)}, bf16[18,2,6144]{2,1,0:T(2,128)(2,1)}, u32[]{:S(2)}, u32[]{:S(2)}) collective-permute-start(bf16[18,2,6144]{2,1,0:T(2,128)(2,1)} %param.3), channel_id=1, source_target_pairs={{0,15},{1,0},{2,1},{3,2},{4,3},{5,4},{6,5},{7,6},{8,7},{9,8},{10,9... | collective-permute-start | bytes 1327112 | tf_op jit(solution)/shard_map/ppermute | solution.py:11
  19.3 1.9 pad_maximum_fusion
  21.2 37.2 %while.1 = (s32[]{:T(128)}, bf16[18,2,13824]{2,1,0:T(2,128)(2,1)S(1)}, s32[18,3]{0,1:T(4,128)S(1)}, bf16[18,2,9984]{2,1,0:T(2,128)(2,1)S(1)}, s32[]{:T(128)}) while((s32[]{:T(128)}, bf16[18,2,13824]{2,1,0:T(2,128)(2,1)S(1)}, s32[18,3]{0,1:T(4,128)S(1)}, bf16[18,2,9984]{2,1,0:T(2,128)(2,1)S(1)}, s32[]{:T(128)}) %tuple.36), condition=%wide.while_cond, body=%wide.while_body.sunk | while | flops 2 | bytes 79997 | solution.py:39
  28.0 1.4 dynamic-slice_dynamic-update-slice_fusion.2
  30.1 1.4 dynamic-slice_dynamic-update-slice_fusion.2
  38.4 1.4 dynamic-slice_dynamic-update-slice_fusion.2
  40.4 1.4 dynamic-slice_dynamic-update-slice_fusion.2
  58.8 3.2 %fusion.1 = bf16[256,18,2,24]{0,3,1,2:T(8,128)(2,1)S(1)} fusion(f32[2,256,2,256,1]{3,2,1,0,4:T(2,128)S(1)} %bitcast.53, f32[18,2,39,256]{3,2,1,0:T(8,128)S(1)} %reshape.56, f32[256]{0:T(256)S(1)} %bitcast.56, f32[256]{0:T(256)S(1)} %bitcast.57, f32[256]{0:T(256)S(1)} %bitcast.58, f32[256]{0:T(256)S(1)} %bitcast.59, f32[256]{0:T(256)S(1)} %bitcast.60, ...), kind=kOutput, calls=%fused_computation.6 | convolution fusion | flops 1366032384 | bytes 15663104 | tf_op jit(solution)/shard_map/icsk,ckdf->fids/dot_general | solution.py:52
  61.9 2.6 %copy.37 = bf16[256,18,2,24]{3,2,1,0:T(2,128)(2,1)S(1)} copy(bf16[256,18,2,24]{0,3,1,2:T(8,128)(2,1)S(1)} %fusion.1) | data formatting | bytes 884736 | tf_op jit(solution)/shard_map/convert_element_type | solution.py:54
  64.6 3.1 %reshape.62 = bf16[32,2,3456]{2,1,0:T(2,128)(2,1)S(1)} reshape(bf16[256,18,2,24]{3,2,1,0:T(2,128)(2,1)S(1)} %copy.37) | data formatting | bytes 884736
  67.7 26.0 %all_to_all.18 = bf16[32,2,3456]{2,1,0:T(2,128)(2,1)S(1)} all-to-all(bf16[32,2,3456]{2,1,0:T(2,128)(2,1)S(1)} %reshape.62), channel_id=1, replica_groups=mesh['inp'=32,'tm'=16] {'inp'}, dimensions={0} | all-to-all | bytes 884736 | tf_op jit(solution)/shard_map/all_to_all | solution.py:55
  93.7 3.3 %reshape.63 = bf16[256,18,2,24]{3,2,1,0:T(2,128)(2,1)S(1)} reshape(bf16[32,2,3456]{2,1,0:T(2,128)(2,1)S(1)} %all_to_all.18) | data formatting | bytes 884736
  97.0 2.0 copy.62
  98.9 7.4 %copy.51 = bf16[8,32,18,2,24]{2,1,0,3,4:T(8,128)(2,1)S(1)} copy(bf16[8,32,18,2,24]{4,0,1,3,2:T(8,128)(2,1)} %bitcast.52) | data formatting | bytes 884736 | tf_op jit(solution)/shard_map/all_to_all | solution.py:55
  106.3 6.5 %reshape.60 = bf16[8,576,2,24]{1,0,2,3:T(8,128)(2,1)} reshape(bf16[8,32,18,2,24]{2,1,0,3,4:T(8,128)(2,1)S(1)} %copy.51) | data formatting | bytes 884736 | tf_op jit(solution)/shard_map/all_to_all | solution.py:55
  112.9 53.9 %all-gather.2.cloned.1.call-done = bf16[8,576,2,384]{1,0,2,3:T(8,128)(2,1)} async-done(((bf16[8,576,2,24]{1,0,2,3:T(8,128)(2,1)}), bf16[8,576,2,384]{1,0,2,3:T(8,128)(2,1)}) %all-gather.2.cloned.1.call-update) | async-done | bytes 7077904 | tf_op jit(solution)/shard_map/all_gather | solution.py:61
  166.8 2.5 %constant_dynamic-slice_fusion.1 = (bf16[8,36,1,384]{1,0,2,3:T(8,128)(2,1)S(1)}, bf16[8,36,1,384]{1,0,2,3:T(8,128)(2,1)S(1)}) fusion(bf16[8,576,2,384]{1,0,2,3:T(8,128)(2,1)} %all-gather.2.cloned.1.call-done, s32[]{:T(128)S(6)} %select_n.21, s32[]{:T(128)S(6)} %add.85), kind=kLoop, calls=%fused_computation.78 | loop fusion | bytes 884744 | tf_op jit(solution)/shard_map/slice | solution.py:66
  170.3 2.5 %constant_dynamic-slice_fusion.2 = bf16[8,36,2,384]{1,0,2,3:T(8,128)(2,1)S(1)} fusion(bf16[8,576,2,384]{1,0,2,3:T(8,128)(2,1)} %all-gather.2.cloned.1.call-done, s32[]{:T(128)S(6)} %select_n.21), kind=kLoop, calls=%fused_computation.79 | loop fusion | bytes 884740 | tf_op jit(solution)/shard_map/dynamic_slice | solution.py:64
  172.8 1.7 copy.52
  174.5 14.8 %copy.43 = bf16[8,576,2,384]{3,2,1,0:T(2,128)(2,1)} copy(bf16[8,576,2,384]{1,0,2,3:T(8,128)(2,1)} %all-gather.2.cloned.1.call-done) | data formatting | bytes 14155776 | tf_op jit(solution)/shard_map/all_gather | solution.py:61
  189.3 16.1 %reshape.32 = bf16[8,576,768]{2,1,0:T(8,128)(2,1)} reshape(bf16[8,576,2,384]{3,2,1,0:T(2,128)(2,1)} %copy.43) | data formatting | bytes 14155776 | tf_op jit(solution)/shard_map/reshape | solution.py:63
  205.7 5.2 %fusion.67 = f32[8,36,576]{2,1,0:T(8,128)S(1)} fusion(bf16[8,36,768]{2,1,0:T(8,128)(2,1)S(1)} %reshape.61, bf16[8,576,768]{2,1,0:T(8,128)(2,1)} %reshape.32), kind=kOutput, calls=%fused_computation.85 | convolution fusion | flops 254803968 | bytes 8183808 | tf_op jit(solution)/shard_map/fas,fbs->fab/dot_general | solution.py:67
  211.0 2.0 fusion.34
  (78 shorter events, 40.5 us)
Async XLA Ops:
  6.5 160.2 %all-gather.2.cloned.1.call-start = ((), (), s32[]{:S(2)}) async-start(), calls=%async_computation.1 | async-start | bytes 8355840 | tf_op jit(solution)/shard_map/all_gather | solution.py:61
  6.5 10.4 %collective-permute-start = (bf16[18,2,6144]{2,1,0:T(2,128)(2,1)}, bf16[18,2,6144]{2,1,0:T(2,128)(2,1)}, u32[]{:S(2)}, u32[]{:S(2)}) collective-permute-start(bf16[18,2,6144]{2,1,0:T(2,128)(2,1)} %param.3), channel_id=1, source_target_pairs={{0,1},{1,2},{2,3},{3,4},{4,5},{5,6},{6,7},{7,8},{8,9},{9,10},{10,1... | collective-permute-start | bytes 1327112 | tf_op jit(solution)/shard_map/ppermute | solution.py:11
  9.2 8.9 %collective-permute-start.1 = (bf16[18,2,6144]{2,1,0:T(2,128)(2,1)}, bf16[18,2,6144]{2,1,0:T(2,128)(2,1)}, u32[]{:S(2)}, u32[]{:S(2)}) collective-permute-start(bf16[18,2,6144]{2,1,0:T(2,128)(2,1)} %param.3), channel_id=1, source_target_pairs={{0,15},{1,0},{2,1},{3,2},{4,3},{5,4},{6,5},{7,6},{8,7},{9,8},{10,9... | collective-permute-start | bytes 1327112 | tf_op jit(solution)/shard_map/ppermute | solution.py:11
  15.4 1.5 copy-start.1
  205.7 5.2 %copy-start = (bf16[8,576,768]{2,1,0:T(8,128)(2,1)S(1)}, bf16[8,576,768]{2,1,0:T(8,128)(2,1)}, u32[]{:S(2)}) copy-start(bf16[8,576,768]{2,1,0:T(8,128)(2,1)} %reshape.32) | copy-start | bytes 21233668
Sparse Core Ops, SparseCore 0:
  113.0 53.7 all-gather.1
where the time goes:
time: 223 us; the launch traced here: 221 us
  local copies, waits for them, and re-layouts  104 us (47%)
  waiting for transfers between devices  53.9 us (24%)
  blocking collectives  26 us (12%)
  between operations  13.6 us (6%)
  matrix products  10.4 us (5%)
  starting transfers between devices  6.84 us (3%)
  other arithmetic  6.02 us (3%)
    all_gather x1, waiting for transfers between devices, shards(): piece = lax.all_gather(turned, 'tm', axis=3, tiled=True)  53.9 us
    gather x54, local copies, waits for them, and re-layouts  36.9 us
    all_to_all x1, blocking collectives, shards(): lax.all_to_all(spectra, 'inp', split_axis=0, concat_axis=1, tiled=True)  26 us
    reshape x1, local copies, waits for them, and re-layouts, shards(): all_rows = piece.reshape(local_channels, all_inputs, 2 * width)  16.1 us
    all_to_all x3, local copies, waits for them, and re-layouts, shards(): lax.all_to_all(spectra, 'inp', split_axis=0, concat_axis=1, tiled=True)  15.8 us
    all_gather x1, local copies, waits for them, and re-layouts, shards(): piece = lax.all_gather(turned, 'tm', axis=3, tiled=True)  14.8 us
    unnamed x9, local copies, waits for them, and re-layouts  7.54 us
    ppermute x2, starting transfers between devices, shifted(): lax.ppermute(value, axis, [(i, (i + by) % peers) for i in range(peers)])  6.84 us
  transfers between devices with their start and end apart: 3, of which 1 were waited for; matrix products, arithmetic and copies ran while one was open for 2% of the time, Pallas kernels for 0%

commit v1 on v0

v1 whole, which is shorter than its diff:
```python
import math

import jax
import jax.numpy as jnp
import numpy as np
from jax import lax
from jax.experimental import pallas as pl
from jax.experimental.layout import Layout, with_layout_constraint
from jax.experimental.pallas import tpu as pltpu
from jax.sharding import Mesh
from jax.sharding import PartitionSpec as P

F32 = jnp.float32
BF16 = jnp.bfloat16
LANES = 128
SEG = 18
PER_ROW = 6
HALO_CHUNKS = 32


ORDER = [(p, y) for p in range(32) for y in range(8)]


def split_bf16(value):
    high = value.astype(BF16)
    return high, (value - high.astype(F32)).astype(BF16)


def dft_tables():
    sample = np.arange(128)
    out = []
    for parity in range(2):
        channel = np.array([8 * p + y for p, y in ORDER if y % 2 == parity])
        phase = (np.outer(channel, sample) % 256) * (2.0 * math.pi / 256)
        cosine, sine = np.cos(phase) / 16.0, np.sin(phase) / 16.0
        out.append([np.concatenate([cosine, sine], 1), np.concatenate([-sine, cosine], 1)])
    table = np.asarray(out).reshape(512, 256).astype(np.float32)
    high = table.astype(BF16)
    low = (table - high.astype(np.float32)).astype(BF16)
    return high, low


def filterbank(delays, own, prev, nxt, taps, high, low, out, series, aligned, coef, fir, filt, spec):
    lane = lax.broadcasted_iota(jnp.int32, (160, LANES), 1)
    row8 = lax.broadcasted_iota(jnp.int32, (8, LANES), 0)
    second = (row8 // 2) % 2 == 1
    for tap in range(16):
        first_half = jnp.broadcast_to(taps[pl.ds(tap, 1), :LANES], (8, LANES))
        second_half = jnp.broadcast_to(taps[pl.ds(tap, 1), LANES:], (8, LANES))
        coef[tap] = jnp.where(second, second_half, first_half).astype(F32) * (1.0 / 4096.0)

    def one(i, carry):
        delay = delays[i]
        chunk = delay // LANES
        turn = delay - chunk * LANES
        series[pl.ds(0, 64), :] = prev[pl.ds(pl.multiple_of(i * 64, 64), 64), :].astype(F32)
        series[pl.ds(64, 96), :] = own[pl.ds(pl.multiple_of(i * 96, 32), 96), :].astype(F32)
        series[pl.ds(160, 64), :] = nxt[pl.ds(pl.multiple_of(i * 64, 64), 64), :].astype(F32)
        here = series[pl.ds(4 + 2 * chunk, 160), :]
        after = series[pl.ds(6 + 2 * chunk, 160), :]
        mixed = jnp.where(lane < turn, after, here)
        aligned[...] = pltpu.roll(mixed, (LANES - turn) % LANES, 1)
        total = jnp.zeros((12, 8, LANES), F32)
        for tap in range(16):
            block = aligned[pl.ds(4 * (15 - tap), 96), :].reshape(12, 8, LANES)
            total = total + coef[tap][None] * block
        fir[...] = total.reshape(96, LANES)
        for comp in range(2):
            for k in range(4):
                low_half = fir[pl.ds(24 * k + comp, PER_ROW, stride=4), :]
                high_half = fir[pl.ds(24 * k + 2 + comp, PER_ROW, stride=4), :]
                rows = pl.ds(LANES * k + i, PER_ROW, stride=SEG)
                filt[comp, rows, :] = low_half + high_half
                filt[2 + comp, rows, :] = low_half - high_half
        return carry

    lax.fori_loop(0, SEG, one, 0)
    contract = (((1,), (1,)), ((), ()))
    for k in range(4):
        rows = pl.ds(LANES * k, LANES)
        for parity in range(2):
            values = jnp.concatenate([filt[2 * parity, rows, :], filt[2 * parity + 1, rows, :]], axis=1)
            vh, vl = split_bf16(values)
            th = high[pl.ds(256 * parity, 256), :]
            tl = low[pl.ds(256 * parity, 256), :]
            result = lax.dot_general(th, vh, contract, preferred_element_type=F32)
            result += lax.dot_general(th, vl, contract, preferred_element_type=F32)
            result += lax.dot_general(tl, vh, contract, preferred_element_type=F32)
            for part in range(2):
                start = parity * 8 + part * 4 + k
                spec[pl.ds(start, 128, stride=16), :] = result[128 * part : 128 * part + 128]
    for piece in range(16):
        rows = pl.ds(128 * piece, 128)
        out[rows, :] = spec[rows, :].astype(BF16)[:, :108]


def correlate(half, got, out, sorted_, rows_v, rows_l):
    def arrange(block, carry):
        for pair in range(4):
            message = got[pl.ds(pl.multiple_of(block * 64 + pair * 16, 16), 16), :].astype(F32)
            for e in range(2):
                start = pl.multiple_of(block * 64, 64) + 2 * pair + e
                sorted_[pl.ds(start, 8, stride=8), :108] = message[8 * e : 8 * e + 8]
        return carry

    lax.fori_loop(0, 64, arrange, 0)
    lane = lax.broadcasted_iota(jnp.int32, (8, LANES), 1)
    mine = half[0]

    def build(dst, count, source_of):
        tiles = -(-count * SEG // LANES)

        def one(pk, carry):
            for s in range(PER_ROW):
                blocks = [[None] * tiles for _ in range(2)]
                for core in range(2):
                    for slot in range(count):
                        start = (core * 32 + source_of(slot)) * 64 + pk * 8
                        piece = sorted_[pl.ds(pl.multiple_of(start, 8), 8), :]
                        shift = (SEG * slot - SEG * s) % LANES
                        piece = pltpu.roll(piece, shift, 1) if shift else piece
                        begin, end = SEG * slot, SEG * slot + SEG
                        for tile in range(begin // LANES, (end - 1) // LANES + 1):
                            lo = max(begin - tile * LANES, 0)
                            old = blocks[core][tile]
                            if old is None:
                                blocks[core][tile] = piece
                            else:
                                blocks[core][tile] = jnp.where(lane < lo, old, piece)
                for tile in range(tiles):
                    both = jnp.concatenate([blocks[0][tile], blocks[1][tile]], axis=0).astype(BF16)
                    start = pl.multiple_of((pk * PER_ROW + s) * 16, 16)
                    dst[pl.ds(start, 16), tile * LANES : tile * LANES + LANES] = both
            return carry

        lax.fori_loop(0, 8, one, 0)

    build(rows_v, 32, lambda slot: slot)
    build(rows_l, 16, lambda slot: 4 * (slot // 2) + 2 * mine + slot % 2)
    contract = (((0,), (0,)), ((), ()))

    def product(left, right):
        return lax.dot_general(
            rows_l[pl.ds(384 * left, 384), :], rows_v[pl.ds(384 * right, 384), :], contract, preferred_element_type=F32
        )

    real = (product(0, 0) + product(1, 1))[:288, :576]
    imag = (product(1, 0) - product(0, 1))[:288, :576]
    both = (jnp.concatenate([real, imag], axis=1) * (1.0 / 384.0))
    for block in range(8):
        for tile in range(9):
            out[block, pl.ds(36 * tile, 36), :] = both[
                36 * block : 36 * block + 36, LANES * tile : LANES * tile + LANES
            ].astype(BF16)


def halves(delays, samples, taps):
    chunks = samples.reshape(SEG, 2, 48, LANES).transpose(0, 2, 1, 3)
    perm = lambda by: [(i, (i + by) % 16) for i in range(16)]
    tail = chunks[:, 48 - HALO_CHUNKS :]
    head = chunks[:, :HALO_CHUNKS]
    prev = lax.ppermute(tail, ("y", "core"), perm(1))
    nxt = lax.ppermute(head, ("y", "core"), perm(-1))
    flat = lambda v: v.reshape(-1, LANES)
    return flat(chunks), flat(prev), flat(nxt)


def run_filterbank(delays, own, prev, nxt, taps, interpret=False):
    high, low = dft_tables()
    smem = pl.BlockSpec(memory_space=pltpu.SMEM)
    vmem = pl.BlockSpec(memory_space=pltpu.VMEM)
    return pl.pallas_call(
        filterbank,
        out_shape=jax.ShapeDtypeStruct((2048, 108), BF16),
        in_specs=[smem] + [vmem] * 6,
        out_specs=vmem,
        scratch_shapes=[
            pltpu.VMEM((232, LANES), F32),
            pltpu.VMEM((160, LANES), F32),
            pltpu.VMEM((16, 8, LANES), F32),
            pltpu.VMEM((96, LANES), F32),
            pltpu.VMEM((4, 512, LANES), F32),
            pltpu.VMEM((2048, LANES), F32),
        ],
        compiler_params=pltpu.CompilerParams(vmem_limit_bytes=48 << 20),
        interpret=interpret,
        name="filterbank",
    )(delays, own, prev, nxt, taps, jnp.asarray(high), jnp.asarray(low))


def run_correlate(half, got, interpret=False):
    smem = pl.BlockSpec(memory_space=pltpu.SMEM)
    vmem = pl.BlockSpec(memory_space=pltpu.VMEM)
    return pl.pallas_call(
        correlate,
        out_shape=jax.ShapeDtypeStruct((8, 324, LANES), BF16),
        in_specs=[smem, vmem],
        out_specs=vmem,
        scratch_shapes=[
            pltpu.VMEM((4096, LANES), F32),
            pltpu.VMEM((768, 640), BF16),
            pltpu.VMEM((768, 384), BF16),
        ],
        compiler_params=pltpu.CompilerParams(vmem_limit_bytes=48 << 20),
        interpret=interpret,
        name="correlate",
    )(half, got)


def row_major(value):
    return with_layout_constraint(value, Layout(tuple(range(value.ndim))))


def finish(rows):
    value = rows.reshape(8, 9, 36, LANES).astype(F32)
    return value.transpose(0, 2, 1, 3).reshape(8, 36, 1152)


def shards(samples, delays, taps):
    own, prev, nxt = halves(delays, samples, taps)
    spectra = run_filterbank(delays, own, prev, nxt, taps)
    turned = lax.all_to_all(spectra.reshape(256, 8, 108), ("inp", "y"), 0, 0, tiled=True)
    turned = row_major(turned.reshape(2048, 108))
    both = row_major(lax.all_gather(turned, "core", axis=0, tiled=True))
    half = lax.axis_index("core").astype(jnp.int32).reshape(1)
    rows = run_correlate(half, both)
    mine = lax.all_to_all(rows, "y", 0, 0, tiled=True)
    return finish(mine)


def solution(mesh):
    fine = Mesh(mesh.devices.reshape(32, 8, 2), ("inp", "y", "core"))
    in_specs = (P("inp", None, ("y", "core")), P("inp"), P())
    out_specs = P("inp", ("y", "core"), None)
    return jax.shard_map(shards, mesh=fine, in_specs=in_specs, out_specs=out_specs, check_vma=False)
```

time: 223 us -> 92.8 us (0.42)
  local copies, waits for them, and re-layouts: 104 us -> 4.26 us
  waiting for transfers between devices: 53.9 us -> 22.2 us
  starting transfers between devices: 6.84 us -> 26 us
  between operations: 13.6 us -> 0.05 us
  Pallas kernels: 0 us -> 10.9 us
  matrix products: 10.4 us -> 0 us
  other arithmetic: 6.02 us -> 0 us
  blocking collectives: 26 us -> 29.1 us
    all_gather x1 -> x0, waiting for transfers between devices: 53.9 us -> none  [shards(): piece = lax.all_gather(turned, 'tm', axis=3, tiled=True)]
    gather x54 -> x0, local copies, waits for them, and re-layouts: 36.9 us -> none
    all_to_all x0 -> x1, starting transfers between devices: none -> 19.2 us  [shards(): lax.all_to_all(spectra.reshape(256, 8, 108), ('inp', 'y'), 0, 0, tiled=True)]
    all_to_all x0 -> x1, waiting for transfers between devices: none -> 18.5 us  [shards(): lax.all_to_all(spectra.reshape(256, 8, 108), ('inp', 'y'), 0, 0, tiled=True)]
    reshape x3 -> x2, local copies, waits for them, and re-layouts: 18.1 us -> 1.24 us  [finish(): return value.transpose(0, 2, 1, 3).reshape(8, 36, 1152)]
    all_to_all x3 -> x0, local copies, waits for them, and re-layouts: 15.8 us -> none  [shards(): lax.all_to_all(spectra, 'inp', split_axis=0, concat_axis=1, tiled=True)]
    all_gather x1 -> x0, local copies, waits for them, and re-layouts: 14.8 us -> none  [shards(): piece = lax.all_gather(turned, 'tm', axis=3, tiled=True)]
    pallas_call x0 -> x2, Pallas kernels: none -> 10.9 us  [the longest x1 5.5 us: run_correlate(): pl.pallas_call(correlate, out_shape=jax.ShapeDtypeStruct((8, 324, LANES),...]
  transfers between devices with their start and end apart: 3 -> 3, of which waited for: 1 -> 3; matrix products, arithmetic and copies ran while one was open for 2% -> 0% of each run, Pallas kernels for 0% -> 0%
where the time goes in v1:
time: 92.8 us; the launch traced here: 92.5 us
  blocking collectives  29.1 us (31%)
  starting transfers between devices  26 us (28%)
  waiting for transfers between devices  22.2 us (24%)
  Pallas kernels  10.9 us (12%)
  local copies, waits for them, and re-layouts  4.26 us (5%)
    all_to_all x1, blocking collectives, shards(): mine = lax.all_to_all(rows, 'y', 0, 0, tiled=True)  23.4 us
    all_to_all x1, starting transfers between devices, shards(): lax.all_to_all(spectra.reshape(256, 8, 108), ('inp', 'y'), 0, 0, tiled=True)  19.2 us
    all_to_all x1, waiting for transfers between devices, shards(): lax.all_to_all(spectra.reshape(256, 8, 108), ('inp', 'y'), 0, 0, tiled=True)  18.5 us
    ppermute x1, starting transfers between devices, halves(): nxt = lax.ppermute(head, ('y', 'core'), perm(-1))  6.84 us
    all_gather x1, blocking collectives, shards(): both = row_major(lax.all_gather(turned, 'core', axis=0, tiled=True))  5.67 us
    pallas_call x1, Pallas kernels, run_correlate(): pl.pallas_call(correlate, out_shape=jax.ShapeDtypeStruct((8, 324, LANES),...  5.5 us
    pallas_call x1, Pallas kernels, run_filterbank(): pl.pallas_call(filterbank, out_shape=jax.ShapeDtypeStruct((2048, 108), BF...  5.38 us
    ppermute x1, waiting for transfers between devices, halves(): prev = lax.ppermute(tail, ('y', 'core'), perm(1))  2.46 us
  transfers between devices with their start and end apart: 3, of which 3 were waited for; matrix products, arithmetic and copies ran while one was open for 0% of the time, Pallas kernels for 0%

profile of v1, /device:TPU:1, one launch (start us, length us, event | category | flops | bytes accessed | tf_op | source)
XLA Modules:
  0.0 92.5 jit_solution(5787780835834333352)
XLA Ops:
  0.0 0.0 copy-start.1
  0.0 0.0 copy-start.2
  0.0 0.0 copy-start
  0.0 1.6 %fusion = (bf16[18,32,2,128]{3,2,1,0:T(2,128)(2,1)S(1)}, bf16[18,32,2,128]{3,2,1,0:T(2,128)(2,1)S(1)}) fusion(bf16[18,48,2,128]{3,2,1,0:T(2,128)(2,1)} %bitcast.16), kind=kLoop, calls=%fused_computation.1 | loop fusion | bytes 1179648 | tf_op jit(solution)/shard_map/slice | solution.py:161
  1.7 6.8 %collective-permute-start.1 = (bf16[18,32,2,128]{3,2,1,0:T(2,128)(2,1)S(1)}, bf16[18,32,2,128]{3,2,1,0:T(2,128)(2,1)S(1)}, u32[]{:S(2)}, u32[]{:S(2)}) collective-permute-start(bf16[18,32,2,128]{3,2,1,0:T(2,128)(2,1)S(1)} %get-tuple-element.5), channel_id=1, source_target_pairs={{0,15},{1,0},{2,1},{3,2},{4,3},{5,4},{6,5},{7,6},{8,7},{9,8},{10,9... | collective-permute-start | bytes 884744 | tf_op jit(solution)/shard_map/ppermute | solution.py:163
  8.5 0.0 collective-permute-start
  8.5 1.2 %collective-permute-done.1 = bf16[18,32,2,128]{3,2,1,0:T(2,128)(2,1)S(1)} collective-permute-done((bf16[18,32,2,128]{3,2,1,0:T(2,128)(2,1)S(1)}, bf16[18,32,2,128]{3,2,1,0:T(2,128)(2,1)S(1)}, u32[]{:S(2)}, u32[]{:S(2)}) %collective-permute-start.1) | collective-permute-done | bytes 294944 | tf_op jit(solution)/shard_map/ppermute | solution.py:163
  9.7 2.5 %collective-permute-done = bf16[18,32,2,128]{3,2,1,0:T(2,128)(2,1)S(1)} collective-permute-done((bf16[18,32,2,128]{3,2,1,0:T(2,128)(2,1)S(1)}, bf16[18,32,2,128]{3,2,1,0:T(2,128)(2,1)S(1)}, u32[]{:S(2)}, u32[]{:S(2)}) %collective-permute-start) | collective-permute-done | bytes 294944 | tf_op jit(solution)/shard_map/ppermute | solution.py:162
  12.2 0.0 copy-done.1
  12.2 0.0 copy-done.2
  12.2 0.0 copy-done
  12.2 0.0 copy-start.3
  12.2 0.7 copy-done.3
  12.9 0.0 copy-start.4
  12.9 0.7 copy-done.4
  13.6 5.4 %filterbank.1 = bf16[2048,108]{1,0:T(8,128)(2,1)} custom-call(s32[18]{0:T(128)S(1)} %copy-done.4, bf16[1728,128]{1,0:T(8,128)(2,1)S(1)} %bitcast.17, bf16[1152,128]{1,0:T(8,128)(2,1)S(1)} %bitcast.19, bf16[1152,128]{1,0:T(8,128)(2,1)S(1)} %bitcast.18, s32[16,256]{1,0:T(8,128)S(1)} %copy-done.3, bf16[512,256]{1,0:T(8,128)(2,1)S(1)} %copy-done.2, ...), custom_call_target="tpu_custom_call" | custom-call | tf_op jit(solution)/shard_map/filterbank/pallas_call | solution.py:172
  18.9 19.2 %all-to-all-start = ((bf16[256,8,108]{2,1,0:T(8,128)(2,1)}), bf16[256,8,108]{2,1,0:T(8,128)(2,1)S(1)}, u32[]{:S(2)}, u32[]{:S(2)}) async-start(bf16[256,8,108]{2,1,0:T(8,128)(2,1)} %bitcast.7), calls=%async_computation | async-start | bytes 1048576 | tf_op jit(solution)/shard_map/all_to_all | solution.py:222
  38.1 18.5 %all-to-all-done = bf16[256,8,108]{2,1,0:T(8,128)(2,1)S(1)} async-done(((bf16[256,8,108]{2,1,0:T(8,128)(2,1)}), bf16[256,8,108]{2,1,0:T(8,128)(2,1)S(1)}, u32[]{:S(2)}, u32[]{:S(2)}) %all-to-all-start) | async-done | bytes 442400 | tf_op jit(solution)/shard_map/all_to_all | solution.py:222
  56.6 5.7 %all_gather.3.got = bf16[4096,108]{1,0:T(8,128)(2,1)S(1)} all-gather(bf16[2048,108]{1,0:T(8,128)(2,1)S(1)} %bitcast.21), channel_id=1, replica_groups=mesh['inp'=32,'y'=8,'core'=2] {'core'}, dimensions={0}, use_global_device_ids=true | all-gather | bytes 1327104 | tf_op jit(solution)/shard_map/all_gather | solution.py:224
  62.3 5.5 %correlate.1 = bf16[8,324,128]{2,1,0:T(8,128)(2,1)S(1)} custom-call(s32[1]{0:T(128)} %bitcast.half, bf16[4096,108]{1,0:T(8,128)(2,1)S(1)} %all_gather.3.got), custom_call_target="tpu_custom_call" | custom-call | tf_op jit(solution)/shard_map/correlate/pallas_call | solution.py:194
  67.8 23.4 %all_to_all.10 = bf16[8,324,128]{2,1,0:T(8,128)(2,1)S(1)} all-to-all(bf16[8,324,128]{2,1,0:T(8,128)(2,1)S(1)} %correlate.1), channel_id=1, replica_groups=mesh['inp'=32,'y'=8,'core'=2] {'y'}, dimensions={0} | all-to-all | bytes 1327104 | tf_op jit(solution)/shard_map/all_to_all | solution.py:227
  91.2 0.1 copy.14
  91.3 1.1 %copy.17 = f32[8,36,9,128]{3,0,2,1:T(8,128)} copy(f32[8,36,9,128]{3,0,1,2:T(8,128)S(1)} %bitcast.20) | data formatting | bytes 2654208 | tf_op jit(solution)/shard_map/reshape | solution.py:216
Async XLA Ops:
  0.0 12.2 %copy-start.1 = (bf16[512,256]{1,0:T(8,128)(2,1)S(1)}, bf16[512,256]{1,0:T(8,128)(2,1)}, u32[]{:S(2)}) copy-start(bf16[512,256]{1,0:T(8,128)(2,1)} %constant.9.clone.low) | copy-start | bytes 786436
  0.0 12.2 %copy-start.2 = (bf16[512,256]{1,0:T(8,128)(2,1)S(1)}, bf16[512,256]{1,0:T(8,128)(2,1)}, u32[]{:S(2)}) copy-start(bf16[512,256]{1,0:T(8,128)(2,1)} %constant.8.clone.high) | copy-start | bytes 786436
  0.0 12.2 %copy-start = (bf16[18,2,6144]{2,1,0:T(2,128)(2,1)S(1)}, bf16[18,2,6144]{2,1,0:T(2,128)(2,1)}, u32[]{:S(2)}) copy-start(bf16[18,2,6144]{2,1,0:T(2,128)(2,1)} %param.5) | copy-start | bytes 1327108
  1.7 8.1 %collective-permute-start.1 = (bf16[18,32,2,128]{3,2,1,0:T(2,128)(2,1)S(1)}, bf16[18,32,2,128]{3,2,1,0:T(2,128)(2,1)S(1)}, u32[]{:S(2)}, u32[]{:S(2)}) collective-permute-start(bf16[18,32,2,128]{3,2,1,0:T(2,128)(2,1)S(1)} %get-tuple-element.5), channel_id=1, source_target_pairs={{0,15},{1,0},{2,1},{3,2},{4,3},{5,4},{6,5},{7,6},{8,7},{9,8},{10,9... | collective-permute-start | bytes 884744 | tf_op jit(solution)/shard_map/ppermute | solution.py:163
  8.5 3.7 %collective-permute-start = (bf16[18,32,2,128]{3,2,1,0:T(2,128)(2,1)S(1)}, bf16[18,32,2,128]{3,2,1,0:T(2,128)(2,1)S(1)}, u32[]{:S(2)}, u32[]{:S(2)}) collective-permute-start(bf16[18,32,2,128]{3,2,1,0:T(2,128)(2,1)S(1)} %get-tuple-element.6), channel_id=1, source_target_pairs={{0,1},{1,2},{2,3},{3,4},{4,5},{5,6},{6,7},{7,8},{8,9},{9,10},{10,1... | collective-permute-start | bytes 884744 | tf_op jit(solution)/shard_map/ppermute | solution.py:162
  12.2 0.7 copy-start.3
  12.9 0.7 copy-start.4
  18.9 37.7 %all-to-all-start = ((bf16[256,8,108]{2,1,0:T(8,128)(2,1)}), bf16[256,8,108]{2,1,0:T(8,128)(2,1)S(1)}, u32[]{:S(2)}, u32[]{:S(2)}) async-start(bf16[256,8,108]{2,1,0:T(8,128)(2,1)} %bitcast.7), calls=%async_computation | async-start | bytes 1048576 | tf_op jit(solution)/shard_map/all_to_all | solution.py:222

commit v2 on v1

--- a/solution.py
+++ b/solution.py
@@ -47,12 +47,11 @@
     for tap in range(16):
         first_half = jnp.broadcast_to(taps[pl.ds(tap, 1), :LANES], (8, LANES))
         second_half = jnp.broadcast_to(taps[pl.ds(tap, 1), LANES:], (8, LANES))
-        coef[tap] = jnp.where(second, second_half, first_half).astype(F32) * (1.0 / 4096.0)
+        coef[tap] = jnp.where(second, second_half, first_half)
 
     def one(i, carry):
-        delay = delays[i]
-        chunk = delay // LANES
-        turn = delay - chunk * LANES
+        chunk = delays[0, i]
+        turn = delays[1, i]
         series[pl.ds(0, 64), :] = prev[pl.ds(pl.multiple_of(i * 64, 64), 64), :].astype(F32)
         series[pl.ds(64, 96), :] = own[pl.ds(pl.multiple_of(i * 96, 32), 96), :].astype(F32)
         series[pl.ds(160, 64), :] = nxt[pl.ds(pl.multiple_of(i * 64, 64), 64), :].astype(F32)
@@ -94,59 +93,57 @@
         out[rows, :] = spec[rows, :].astype(BF16)[:, :108]
 
 
-def correlate(half, got, out, sorted_, rows_v, rows_l):
-    def arrange(block, carry):
-        for pair in range(4):
-            message = got[pl.ds(pl.multiple_of(block * 64 + pair * 16, 16), 16), :].astype(F32)
-            for e in range(2):
-                start = pl.multiple_of(block * 64, 64) + 2 * pair + e
-                sorted_[pl.ds(start, 8, stride=8), :108] = message[8 * e : 8 * e + 8]
+def correlate(half, got, out, rows_v, rows_l):
+    lane = lax.broadcasted_iota(jnp.int32, (16, LANES), 1)
+    sign = jnp.where(lax.broadcasted_iota(jnp.int32, (8, LANES), 0) < 4, 1.0, -1.0)
+    mine = half[0]
+
+    def gather_lanes(dst, group, pieces):
+        turned = {}
+        for diff in range(1 - PER_ROW, 32):
+            merged = None
+            for s in range(PER_ROW):
+                if 0 <= diff + s < 32:
+                    piece = pieces[diff + s]
+                    merged = piece if merged is None else jnp.where(lane < SEG * s, merged, piece)
+            shift = (SEG * diff) % LANES
+            turned[diff] = pltpu.roll(merged, shift, 1) if shift else merged
+        for s in range(PER_ROW):
+            tiles = [None] * 5
+            for slot in range(32):
+                begin, end = SEG * slot, SEG * slot + SEG
+                for tile in range(begin // LANES, (end - 1) // LANES + 1):
+                    new = turned[slot - s]
+                    old = tiles[tile]
+                    tiles[tile] = new if old is None else jnp.where(lane < begin - tile * LANES, old, new)
+            for tile in range(5):
+                rows = pl.ds(pl.multiple_of((group * PER_ROW + s) * 16, 16), 16)
+                dst[rows, tile * LANES : tile * LANES + LANES] = tiles[tile].astype(BF16)
+
+    def piece_at(group, p):
+        core, pair = group // 4, group % 4
+        start = pl.multiple_of(core * 2048 + p * 64 + pair * 16, 16)
+        return pad(got[pl.ds(start, 16), :])
+
+    def pad(piece):
+        return jnp.concatenate([piece, jnp.zeros((16, LANES - 108), BF16)], axis=1)
+
+    def swapped(piece):
+        value = piece.astype(F32)
+        parts = [pltpu.roll(value[8 * e : 8 * e + 8], 4, 0) * sign for e in range(2)]
+        return jnp.concatenate(parts, axis=0).astype(BF16)
+
+    def one(group, carry):
+        gather_lanes(rows_v, group, [piece_at(group, p) for p in range(32)])
+        own = [piece_at(group, 4 * (u // 2) + 2 * mine + u % 2) for u in range(16)]
+        gather_lanes(rows_l, group, own + [swapped(piece) for piece in own])
         return carry
 
-    lax.fori_loop(0, 64, arrange, 0)
-    lane = lax.broadcasted_iota(jnp.int32, (8, LANES), 1)
-    mine = half[0]
-
-    def build(dst, count, source_of):
-        tiles = -(-count * SEG // LANES)
-
-        def one(pk, carry):
-            for s in range(PER_ROW):
-                blocks = [[None] * tiles for _ in range(2)]
-                for core in range(2):
-                    for slot in range(count):
-                        start = (core * 32 + source_of(slot)) * 64 + pk * 8
-                        piece = sorted_[pl.ds(pl.multiple_of(start, 8), 8), :]
-                        shift = (SEG * slot - SEG * s) % LANES
-                        piece = pltpu.roll(piece, shift, 1) if shift else piece
-                        begin, end = SEG * slot, SEG * slot + SEG
-                        for tile in range(begin // LANES, (end - 1) // LANES + 1):
-                            lo = max(begin - tile * LANES, 0)
-                            old = blocks[core][tile]
-                            if old is None:
-                                blocks[core][tile] = piece
-                            else:
-                                blocks[core][tile] = jnp.where(lane < lo, old, piece)
-                for tile in range(tiles):
-                    both = jnp.concatenate([blocks[0][tile], blocks[1][tile]], axis=0).astype(BF16)
-                    start = pl.multiple_of((pk * PER_ROW + s) * 16, 16)
-                    dst[pl.ds(start, 16), tile * LANES : tile * LANES + LANES] = both
-            return carry
-
-        lax.fori_loop(0, 8, one, 0)
-
-    build(rows_v, 32, lambda slot: slot)
-    build(rows_l, 16, lambda slot: 4 * (slot // 2) + 2 * mine + slot % 2)
-    contract = (((0,), (0,)), ((), ()))
-
-    def product(left, right):
-        return lax.dot_general(
-            rows_l[pl.ds(384 * left, 384), :], rows_v[pl.ds(384 * right, 384), :], contract, preferred_element_type=F32
-        )
-
-    real = (product(0, 0) + product(1, 1))[:288, :576]
-    imag = (product(1, 0) - product(0, 1))[:288, :576]
-    both = (jnp.concatenate([real, imag], axis=1) * (1.0 / 384.0))
+    lax.fori_loop(0, 8, one, 0)
+    gram = lax.dot_general(
+        rows_l[...], rows_v[...], (((0,), (0,)), ((), ())), preferred_element_type=F32
+    ) * (1.0 / 384.0)
+    both = jnp.concatenate([gram[:288, :576], gram[288:576, :576]], axis=1)
     for block in range(8):
         for tile in range(9):
             out[block, pl.ds(36 * tile, 36), :] = both[
@@ -154,15 +151,12 @@
             ].astype(BF16)
 
 
-def halves(delays, samples, taps):
-    chunks = samples.reshape(SEG, 2, 48, LANES).transpose(0, 2, 1, 3)
-    perm = lambda by: [(i, (i + by) % 16) for i in range(16)]
-    tail = chunks[:, 48 - HALO_CHUNKS :]
-    head = chunks[:, :HALO_CHUNKS]
-    prev = lax.ppermute(tail, ("y", "core"), perm(1))
-    nxt = lax.ppermute(head, ("y", "core"), perm(-1))
-    flat = lambda v: v.reshape(-1, LANES)
-    return flat(chunks), flat(prev), flat(nxt)
+def with_neighbours(samples):
+    chunks = samples.reshape(SEG, 2, 48, LANES).transpose(0, 2, 1, 3).reshape(SEG, 96, LANES)
+    ring = lambda by: [(i, (i + by) % 16) for i in range(16)]
+    prev = lax.ppermute(chunks[:, 32:], ("y", "core"), ring(1))
+    nxt = lax.ppermute(chunks[:, :64], ("y", "core"), ring(-1))
+    return [v.reshape(-1, LANES) for v in (chunks, prev, nxt)]
 
 
 def run_filterbank(delays, own, prev, nxt, taps, interpret=False):
@@ -197,9 +191,8 @@
         in_specs=[smem, vmem],
         out_specs=vmem,
         scratch_shapes=[
-            pltpu.VMEM((4096, LANES), F32),
             pltpu.VMEM((768, 640), BF16),
-            pltpu.VMEM((768, 384), BF16),
+            pltpu.VMEM((768, 640), BF16),
         ],
         compiler_params=pltpu.CompilerParams(vmem_limit_bytes=48 << 20),
         interpret=interpret,
@@ -217,8 +210,10 @@
 
 
 def shards(samples, delays, taps):
-    own, prev, nxt = halves(delays, samples, taps)
-    spectra = run_filterbank(delays, own, prev, nxt, taps)
+    own, prev, nxt = with_neighbours(samples)
+    split = jnp.stack([delays // LANES, delays % LANES])
+    coefficient = taps.astype(F32) * (1.0 / 4096.0)
+    spectra = run_filterbank(split, own, prev, nxt, coefficient)
     turned = lax.all_to_all(spectra.reshape(256, 8, 108), ("inp", "y"), 0, 0, tiled=True)
     turned = row_major(turned.reshape(2048, 108))
     both = row_major(lax.all_gather(turned, "core", axis=0, tiled=True))

time: 92.8 us -> 88.4 us (0.953)
  Pallas kernels: 10.9 us -> 8.33 us
  local copies, waits for them, and re-layouts: 4.26 us -> 2.43 us
  other arithmetic: 0 us -> 1.4 us
  waiting for transfers between devices: 22.2 us -> 20.8 us
    pallas_call x1, Pallas kernels: 5.5 us -> 2.92 us  [run_correlate(): pl.pallas_call(correlate, out_shape=jax.ShapeDtypeStruct((8, 324, LANES),...]
    ppermute x2, waiting for transfers between devices: 3.67 us -> 2.27 us  [the longest x1 2.27 us: with_neighbours(): prev = lax.ppermute(chunks[:, 32:], ('y', 'core'), ring(1))]
    unnamed x10 -> x6, local copies, waits for them, and re-layouts: 1.38 us -> 0.01 us
  transfers between devices with their start and end apart: 3 -> 3, of which waited for: 3 -> 2; matrix products, arithmetic and copies ran while one was open for 0% -> 2% of each run, Pallas kernels for 0% -> 0%
where the time goes in v2:
time: 88.4 us; the launch traced here: 88.1 us
  blocking collectives  29.1 us (33%)
  starting transfers between devices  26 us (29%)
  waiting for transfers between devices  20.8 us (24%)
  Pallas kernels  8.33 us (9%)
  local copies, waits for them, and re-layouts  2.43 us (3%)
  other arithmetic  1.4 us (2%)
    all_to_all x1, blocking collectives, shards(): mine = lax.all_to_all(rows, 'y', 0, 0, tiled=True)  23.4 us
    all_to_all x1, starting transfers between devices, shards(): lax.all_to_all(spectra.reshape(256, 8, 108), ('inp', 'y'), 0, 0, tiled=True)  19.1 us
    all_to_all x1, waiting for transfers between devices, shards(): lax.all_to_all(spectra.reshape(256, 8, 108), ('inp', 'y'), 0, 0, tiled=True)  18.5 us
    ppermute x1, starting transfers between devices, with_neighbours(): nxt = lax.ppermute(chunks[:, :64], ('y', 'core'), ring(-1))  6.84 us
    all_gather x1, blocking collectives, shards(): both = row_major(lax.all_gather(turned, 'core', axis=0, tiled=True))  5.68 us
    pallas_call x1, Pallas kernels, run_filterbank(): pl.pallas_call(filterbank, out_shape=jax.ShapeDtypeStruct((2048, 108), BF...  5.42 us
    pallas_call x1, Pallas kernels, run_correlate(): pl.pallas_call(correlate, out_shape=jax.ShapeDtypeStruct((8, 324, LANES),...  2.92 us
    ppermute x1, waiting for transfers between devices, with_neighbours(): prev = lax.ppermute(chunks[:, 32:], ('y', 'core'), ring(1))  2.27 us
  transfers between devices with their start and end apart: 3, of which 2 were waited for; matrix products, arithmetic and copies ran while one was open for 2% of the time, Pallas kernels for 0%

profile of v2, /device:TPU:1, one launch (start us, length us, event | category | flops | bytes accessed | tf_op | source)
XLA Modules:
  0.0 88.1 jit_solution(6288033116087210448)
XLA Ops:
  0.0 0.0 copy-start.1
  0.0 0.0 copy-start.2
  0.0 0.0 copy-start
  0.0 1.2 %fusion.2 = (bf16[18,64,128]{2,1,0:T(8,128)(2,1)S(1)}, bf16[18,64,128]{2,1,0:T(8,128)(2,1)S(1)}) fusion(bf16[18,96,128]{2,1,0:T(8,128)(2,1)} %bitcast.22), kind=kLoop, calls=%fused_computation.10 | loop fusion | bytes 1179648 | tf_op jit(solution)/shard_map/slice | solution.py:158
  1.2 6.8 %collective-permute-start.1 = (bf16[18,64,128]{2,1,0:T(8,128)(2,1)S(1)}, bf16[18,64,128]{2,1,0:T(8,128)(2,1)S(1)}, u32[]{:S(2)}, u32[]{:S(2)}) collective-permute-start(bf16[18,64,128]{2,1,0:T(8,128)(2,1)S(1)} %get-tuple-element.5), channel_id=1, source_target_pairs={{0,15},{1,0},{2,1},{3,2},{4,3},{5,4},{6,5},{7,6},{8,7},{9,8},{10,9... | collective-permute-start | bytes 884744 | tf_op jit(solution)/shard_map/ppermute | solution.py:158
  8.0 0.0 collective-permute-start
  8.0 0.7 fusion.1
  8.7 0.7 convert_multiply_fusion.taps
  9.4 0.0 collective-permute-done.1
  9.4 2.3 %collective-permute-done = bf16[18,64,128]{2,1,0:T(8,128)(2,1)S(1)} collective-permute-done((bf16[18,64,128]{2,1,0:T(8,128)(2,1)S(1)}, bf16[18,64,128]{2,1,0:T(8,128)(2,1)S(1)}, u32[]{:S(2)}, u32[]{:S(2)}) %collective-permute-start) | collective-permute-done | bytes 294944 | tf_op jit(solution)/shard_map/ppermute | solution.py:157
  11.7 0.0 copy-done.1
  11.7 0.0 copy-done.2
  11.7 0.0 copy-done
  11.7 5.4 %filterbank.1 = bf16[2048,108]{1,0:T(8,128)(2,1)} custom-call(s32[2,18]{1,0:T(2,128)S(1)} %pad_add_fusion.delays, bf16[1728,128]{1,0:T(8,128)(2,1)S(1)} %bitcast.23, bf16[1152,128]{1,0:T(8,128)(2,1)S(1)} %bitcast.25, bf16[1152,128]{1,0:T(8,128)(2,1)S(1)} %bitcast.24, f32[16,256]{1,0:T(8,128)S(1)} %convert_multiply_fusion.taps, ...), custom_call_target="tpu_custom_call" | custom-call | tf_op jit(solution)/shard_map/filterbank/pallas_call | solution.py:166
  17.1 19.1 %all-to-all-start = ((bf16[256,8,108]{2,1,0:T(8,128)(2,1)}), bf16[256,8,108]{2,1,0:T(8,128)(2,1)S(1)}, u32[]{:S(2)}, u32[]{:S(2)}) async-start(bf16[256,8,108]{2,1,0:T(8,128)(2,1)} %bitcast.11), calls=%async_computation | async-start | bytes 1048576 | tf_op jit(solution)/shard_map/all_to_all | solution.py:217
  36.3 18.5 %all-to-all-done = bf16[256,8,108]{2,1,0:T(8,128)(2,1)S(1)} async-done(((bf16[256,8,108]{2,1,0:T(8,128)(2,1)}), bf16[256,8,108]{2,1,0:T(8,128)(2,1)S(1)}, u32[]{:S(2)}, u32[]{:S(2)}) %all-to-all-start) | async-done | bytes 442400 | tf_op jit(solution)/shard_map/all_to_all | solution.py:217
  54.8 5.7 %all_gather.3.got = bf16[4096,108]{1,0:T(8,128)(2,1)S(1)} all-gather(bf16[2048,108]{1,0:T(8,128)(2,1)S(1)} %bitcast.27), channel_id=1, replica_groups=mesh['inp'=32,'y'=8,'core'=2] {'core'}, dimensions={0}, use_global_device_ids=true | all-gather | bytes 1327104 | tf_op jit(solution)/shard_map/all_gather | solution.py:219
  60.5 2.9 %correlate.1 = bf16[8,324,128]{2,1,0:T(8,128)(2,1)S(1)} custom-call(s32[1]{0:T(128)} %bitcast.half, bf16[4096,108]{1,0:T(8,128)(2,1)S(1)} %all_gather.3.got), custom_call_target="tpu_custom_call" | custom-call | tf_op jit(solution)/shard_map/correlate/pallas_call | solution.py:188
  63.4 23.4 %all_to_all.10 = bf16[8,324,128]{2,1,0:T(8,128)(2,1)S(1)} all-to-all(bf16[8,324,128]{2,1,0:T(8,128)(2,1)S(1)} %correlate.1), channel_id=1, replica_groups=mesh['inp'=32,'y'=8,'core'=2] {'y'}, dimensions={0} | all-to-all | bytes 1327104 | tf_op jit(solution)/shard_map/all_to_all | solution.py:222
  86.8 0.1 copy.14
  86.9 1.1 %copy.17 = f32[8,36,9,128]{3,0,2,1:T(8,128)} copy(f32[8,36,9,128]{3,0,1,2:T(8,128)S(1)} %bitcast.26) | data formatting | bytes 2654208 | tf_op jit(solution)/shard_map/reshape | solution.py:209
  (1 shorter events, 0.0 us)
Async XLA Ops:
  0.0 11.7 %copy-start.1 = (bf16[512,256]{1,0:T(8,128)(2,1)S(1)}, bf16[512,256]{1,0:T(8,128)(2,1)}, u32[]{:S(2)}) copy-start(bf16[512,256]{1,0:T(8,128)(2,1)} %constant.39.clone.low) | copy-start | bytes 786436
  0.0 11.7 %copy-start.2 = (bf16[512,256]{1,0:T(8,128)(2,1)S(1)}, bf16[512,256]{1,0:T(8,128)(2,1)}, u32[]{:S(2)}) copy-start(bf16[512,256]{1,0:T(8,128)(2,1)} %constant.38.clone.high) | copy-start | bytes 786436
  0.0 11.7 %copy-start = (bf16[18,2,6144]{2,1,0:T(2,128)(2,1)S(1)}, bf16[18,2,6144]{2,1,0:T(2,128)(2,1)}, u32[]{:S(2)}) copy-start(bf16[18,2,6144]{2,1,0:T(2,128)(2,1)} %param.5) | copy-start | bytes 1327108
  1.2 8.2 %collective-permute-start.1 = (bf16[18,64,128]{2,1,0:T(8,128)(2,1)S(1)}, bf16[18,64,128]{2,1,0:T(8,128)(2,1)S(1)}, u32[]{:S(2)}, u32[]{:S(2)}) collective-permute-start(bf16[18,64,128]{2,1,0:T(8,128)(2,1)S(1)} %get-tuple-element.5), channel_id=1, source_target_pairs={{0,15},{1,0},{2,1},{3,2},{4,3},{5,4},{6,5},{7,6},{8,7},{9,8},{10,9... | collective-permute-start | bytes 884744 | tf_op jit(solution)/shard_map/ppermute | solution.py:158
  8.0 3.7 %collective-permute-start = (bf16[18,64,128]{2,1,0:T(8,128)(2,1)S(1)}, bf16[18,64,128]{2,1,0:T(8,128)(2,1)S(1)}, u32[]{:S(2)}, u32[]{:S(2)}) collective-permute-start(bf16[18,64,128]{2,1,0:T(8,128)(2,1)S(1)} %get-tuple-element.6), channel_id=1, source_target_pairs={{0,1},{1,2},{2,3},{3,4},{4,5},{5,6},{6,7},{7,8},{8,9},{9,10},{10,1... | collective-permute-start | bytes 884744 | tf_op jit(solution)/shard_map/ppermute | solution.py:157
  17.1 37.7 %all-to-all-start = ((bf16[256,8,108]{2,1,0:T(8,128)(2,1)}), bf16[256,8,108]{2,1,0:T(8,128)(2,1)S(1)}, u32[]{:S(2)}, u32[]{:S(2)}) async-start(bf16[256,8,108]{2,1,0:T(8,128)(2,1)} %bitcast.11), calls=%async_computation | async-start | bytes 1048576 | tf_op jit(solution)/shard_map/all_to_all | solution.py:217

commit v3 on v2

--- a/solution.py
+++ b/solution.py
@@ -16,9 +16,19 @@
 SEG = 18
 PER_ROW = 6
 HALO_CHUNKS = 32
-
-
-ORDER = [(p, y) for p in range(32) for y in range(8)]
+AT_ONCE = 6
+
+
+def exchange_order():
+    pairs = [(p, y) for p in range(32) for y in range(0, 8, 2)]
+    shuffled = [pairs[i] for i in np.random.RandomState(0).permutation(128)]
+    return [(p, y + e) for p, y in shuffled for e in range(2)]
+
+
+ORDER = exchange_order()
+GROUP = [[8 * p + y for p, y in ORDER]]
+PAIR_AT = np.asarray([ORDER.index((p, 2 * j)) // 2 for j in range(4) for p in range(32)], np.int32)
+ROWS_TO = [0, 3, 6, 1, 4, 7, 2, 5]
 
 
 def split_bf16(value):
@@ -49,31 +59,35 @@
         second_half = jnp.broadcast_to(taps[pl.ds(tap, 1), LANES:], (8, LANES))
         coef[tap] = jnp.where(second, second_half, first_half)
 
-    def one(i, carry):
+    def one(i, u):
         chunk = delays[0, i]
         turn = delays[1, i]
-        series[pl.ds(0, 64), :] = prev[pl.ds(pl.multiple_of(i * 64, 64), 64), :].astype(F32)
-        series[pl.ds(64, 96), :] = own[pl.ds(pl.multiple_of(i * 96, 32), 96), :].astype(F32)
-        series[pl.ds(160, 64), :] = nxt[pl.ds(pl.multiple_of(i * 64, 64), 64), :].astype(F32)
-        here = series[pl.ds(4 + 2 * chunk, 160), :]
-        after = series[pl.ds(6 + 2 * chunk, 160), :]
+        series[u, pl.ds(0, 64), :] = prev[pl.ds(pl.multiple_of(i * 64, 64), 64), :].astype(F32)
+        series[u, pl.ds(64, 96), :] = own[pl.ds(pl.multiple_of(i * 96, 32), 96), :].astype(F32)
+        series[u, pl.ds(160, 64), :] = nxt[pl.ds(pl.multiple_of(i * 64, 64), 64), :].astype(F32)
+        here = series[u, pl.ds(4 + 2 * chunk, 160), :]
+        after = series[u, pl.ds(6 + 2 * chunk, 160), :]
         mixed = jnp.where(lane < turn, after, here)
-        aligned[...] = pltpu.roll(mixed, (LANES - turn) % LANES, 1)
+        aligned[u] = pltpu.roll(mixed, (LANES - turn) % LANES, 1)
         total = jnp.zeros((12, 8, LANES), F32)
         for tap in range(16):
-            block = aligned[pl.ds(4 * (15 - tap), 96), :].reshape(12, 8, LANES)
+            block = aligned[u, pl.ds(4 * (15 - tap), 96), :].reshape(12, 8, LANES)
             total = total + coef[tap][None] * block
-        fir[...] = total.reshape(96, LANES)
+        fir[u] = total.reshape(96, LANES)
         for comp in range(2):
             for k in range(4):
-                low_half = fir[pl.ds(24 * k + comp, PER_ROW, stride=4), :]
-                high_half = fir[pl.ds(24 * k + 2 + comp, PER_ROW, stride=4), :]
+                low_half = fir[u, pl.ds(24 * k + comp, PER_ROW, stride=4), :]
+                high_half = fir[u, pl.ds(24 * k + 2 + comp, PER_ROW, stride=4), :]
                 rows = pl.ds(LANES * k + i, PER_ROW, stride=SEG)
                 filt[comp, rows, :] = low_half + high_half
                 filt[2 + comp, rows, :] = low_half - high_half
+
+    def some(step, carry):
+        for u in range(AT_ONCE):
+            one(step * AT_ONCE + u, u)
         return carry
 
-    lax.fori_loop(0, SEG, one, 0)
+    lax.fori_loop(0, SEG // AT_ONCE, some, 0)
     contract = (((1,), (1,)), ((), ()))
     for k in range(4):
         rows = pl.ds(LANES * k, LANES)
@@ -93,7 +107,7 @@
         out[rows, :] = spec[rows, :].astype(BF16)[:, :108]
 
 
-def correlate(half, got, out, rows_v, rows_l):
+def correlate(half, pair_at, got, out, rows_v, rows_l):
     lane = lax.broadcasted_iota(jnp.int32, (16, LANES), 1)
     sign = jnp.where(lax.broadcasted_iota(jnp.int32, (8, LANES), 0) < 4, 1.0, -1.0)
     mine = half[0]
@@ -122,7 +136,7 @@
 
     def piece_at(group, p):
         core, pair = group // 4, group % 4
-        start = pl.multiple_of(core * 2048 + p * 64 + pair * 16, 16)
+        start = pl.multiple_of(core * 2048 + pair_at[pair * 32 + p] * 16, 16)
         return pad(got[pl.ds(start, 16), :])
 
     def pad(piece):
@@ -144,9 +158,9 @@
         rows_l[...], rows_v[...], (((0,), (0,)), ((), ())), preferred_element_type=F32
     ) * (1.0 / 384.0)
     both = jnp.concatenate([gram[:288, :576], gram[288:576, :576]], axis=1)
-    for block in range(8):
+    for place, block in enumerate(ROWS_TO):
         for tile in range(9):
-            out[block, pl.ds(36 * tile, 36), :] = both[
+            out[place, pl.ds(36 * tile, 36), :] = both[
                 36 * block : 36 * block + 36, LANES * tile : LANES * tile + LANES
             ].astype(BF16)
 
@@ -169,10 +183,10 @@
         in_specs=[smem] + [vmem] * 6,
         out_specs=vmem,
         scratch_shapes=[
-            pltpu.VMEM((232, LANES), F32),
-            pltpu.VMEM((160, LANES), F32),
+            pltpu.VMEM((AT_ONCE, 232, LANES), F32),
+            pltpu.VMEM((AT_ONCE, 160, LANES), F32),
             pltpu.VMEM((16, 8, LANES), F32),
-            pltpu.VMEM((96, LANES), F32),
+            pltpu.VMEM((AT_ONCE, 96, LANES), F32),
             pltpu.VMEM((4, 512, LANES), F32),
             pltpu.VMEM((2048, LANES), F32),
         ],
@@ -182,13 +196,13 @@
     )(delays, own, prev, nxt, taps, jnp.asarray(high), jnp.asarray(low))
 
 
-def run_correlate(half, got, interpret=False):
+def run_correlate(half, pair_at, got, interpret=False):
     smem = pl.BlockSpec(memory_space=pltpu.SMEM)
     vmem = pl.BlockSpec(memory_space=pltpu.VMEM)
     return pl.pallas_call(
         correlate,
         out_shape=jax.ShapeDtypeStruct((8, 324, LANES), BF16),
-        in_specs=[smem, vmem],
+        in_specs=[smem, smem, vmem],
         out_specs=vmem,
         scratch_shapes=[
             pltpu.VMEM((768, 640), BF16),
@@ -197,7 +211,7 @@
         compiler_params=pltpu.CompilerParams(vmem_limit_bytes=48 << 20),
         interpret=interpret,
         name="correlate",
-    )(half, got)
+    )(half, pair_at, got)
 
 
 def row_major(value):
@@ -205,21 +219,23 @@
 
 
 def finish(rows):
+    rows = jnp.stack([rows[ROWS_TO.index(channel)] for channel in range(8)])
     value = rows.reshape(8, 9, 36, LANES).astype(F32)
     return value.transpose(0, 2, 1, 3).reshape(8, 36, 1152)
 
 
 def shards(samples, delays, taps):
     own, prev, nxt = with_neighbours(samples)
+    half = lax.axis_index("core").astype(jnp.int32).reshape(1)
     split = jnp.stack([delays // LANES, delays % LANES])
+    split, half, pair_at = lax.optimization_barrier((split, half, jnp.asarray(PAIR_AT)))
     coefficient = taps.astype(F32) * (1.0 / 4096.0)
     spectra = run_filterbank(split, own, prev, nxt, coefficient)
-    turned = lax.all_to_all(spectra.reshape(256, 8, 108), ("inp", "y"), 0, 0, tiled=True)
+    turned = lax.all_to_all(spectra.reshape(256, 8, 108), ("inp", "y"), 0, 0, axis_index_groups=GROUP, tiled=True)
     turned = row_major(turned.reshape(2048, 108))
     both = row_major(lax.all_gather(turned, "core", axis=0, tiled=True))
-    half = lax.axis_index("core").astype(jnp.int32).reshape(1)
-    rows = run_correlate(half, both)
-    mine = lax.all_to_all(rows, "y", 0, 0, tiled=True)
+    rows = run_correlate(half, pair_at, both)
+    mine = lax.all_to_all(rows, "y", 0, 0, axis_index_groups=[ROWS_TO], tiled=True)
     return finish(mine)
 
 

time: 88.4 us -> 84.5 us (0.956)
  blocking collectives: 29.1 us -> 63.1 us
  starting transfers between devices: 26 us -> 6.85 us
  waiting for transfers between devices: 20.8 us -> 2.27 us
  Pallas kernels: 8.33 us -> 7.02 us
    all_to_all x1 -> x2, blocking collectives: 23.4 us -> 57.2 us  [the longest x1 35.2 us: shards(): lax.all_to_all(spectra.reshape(256, 8, 108), ('inp', 'y'), 0, 0, axis_ind...]
    all_to_all x1 -> x0, starting transfers between devices: 19.1 us -> none  [shards(): lax.all_to_all(spectra.reshape(256, 8, 108), ('inp', 'y'), 0, 0, tiled=True)]
    all_to_all x1 -> x0, waiting for transfers between devices: 18.5 us -> none  [shards(): lax.all_to_all(spectra.reshape(256, 8, 108), ('inp', 'y'), 0, 0, tiled=True)]
    pallas_call x1, Pallas kernels: 5.42 us -> 3.33 us  [run_filterbank(): pl.pallas_call(filterbank, out_shape=jax.ShapeDtypeStruct((2048, 108), BF...]
  transfers between devices with their start and end apart: 3 -> 2, of which waited for: 2 -> 1; matrix products, arithmetic and copies ran while one was open for 2% -> 2% of each run, Pallas kernels for 0% -> 0%
where the time goes in v3:
time: 84.5 us; the launch traced here: 83.3 us
  blocking collectives  63.1 us (75%)
  Pallas kernels  7.02 us (8%)
  starting transfers between devices  6.85 us (8%)
  local copies, waits for them, and re-layouts  2.54 us (3%)
  waiting for transfers between devices  2.27 us (3%)
  other arithmetic  1.4 us (2%)
    all_to_all x1, blocking collectives, shards(): lax.all_to_all(spectra.reshape(256, 8, 108), ('inp', 'y'), 0, 0, axis_ind...  35.2 us
    all_to_all x1, blocking collectives, shards(): lax.all_to_all(rows, 'y', 0, 0, axis_index_groups=[ROWS_TO], tiled=True)  22.1 us
    ppermute x1, starting transfers between devices, with_neighbours(): nxt = lax.ppermute(chunks[:, :64], ('y', 'core'), ring(-1))  6.84 us
    all_gather x1, blocking collectives, shards(): both = row_major(lax.all_gather(turned, 'core', axis=0, tiled=True))  5.92 us
    pallas_call x1, Pallas kernels, run_correlate(): pl.pallas_call(correlate, out_shape=jax.ShapeDtypeStruct((8, 324, LANES),...  3.69 us
    pallas_call x1, Pallas kernels, run_filterbank(): pl.pallas_call(filterbank, out_shape=jax.ShapeDtypeStruct((2048, 108), BF...  3.33 us
    ppermute x1, waiting for transfers between devices, with_neighbours(): prev = lax.ppermute(chunks[:, 32:], ('y', 'core'), ring(1))  2.27 us
  transfers between devices with their start and end apart: 2, of which 1 were waited for; matrix products, arithmetic and copies ran while one was open for 2% of the time, Pallas kernels for 0%

profile of v3, /device:TPU:1, one launch (start us, length us, event | category | flops | bytes accessed | tf_op | source)
XLA Modules:
  0.0 83.3 jit_solution(14715226694756246279)
XLA Ops:
  0.0 0.0 copy-start.1
  0.0 0.0 copy-start.2
  0.0 0.0 copy-start
  0.0 1.2 %fusion.2 = (bf16[18,64,128]{2,1,0:T(8,128)(2,1)S(1)}, bf16[18,64,128]{2,1,0:T(8,128)(2,1)S(1)}) fusion(bf16[18,96,128]{2,1,0:T(8,128)(2,1)} %bitcast.22), kind=kLoop, calls=%fused_computation.18 | loop fusion | bytes 1179648 | tf_op jit(solution)/shard_map/slice | solution.py:172
  1.2 6.8 %collective-permute-start.1 = (bf16[18,64,128]{2,1,0:T(8,128)(2,1)S(1)}, bf16[18,64,128]{2,1,0:T(8,128)(2,1)S(1)}, u32[]{:S(2)}, u32[]{:S(2)}) collective-permute-start(bf16[18,64,128]{2,1,0:T(8,128)(2,1)S(1)} %get-tuple-element.11), channel_id=1, source_target_pairs={{0,15},{1,0},{2,1},{3,2},{4,3},{5,4},{6,5},{7,6},{8,7},{9,8},{10,9... | collective-permute-start | bytes 884744 | tf_op jit(solution)/shard_map/ppermute | solution.py:172
  8.0 0.0 collective-permute-start
  8.0 0.7 fusion.1
  8.7 0.7 convert_multiply_fusion.taps
  9.4 0.0 collective-permute-done.1
  9.4 2.3 %collective-permute-done = bf16[18,64,128]{2,1,0:T(8,128)(2,1)S(1)} collective-permute-done((bf16[18,64,128]{2,1,0:T(8,128)(2,1)S(1)}, bf16[18,64,128]{2,1,0:T(8,128)(2,1)S(1)}, u32[]{:S(2)}, u32[]{:S(2)}) %collective-permute-start) | collective-permute-done | bytes 294944 | tf_op jit(solution)/shard_map/ppermute | solution.py:171
  11.7 0.0 copy-done.1
  11.7 0.0 copy-done.2
  11.7 0.0 copy-done
  11.7 3.3 %filterbank.1 = bf16[2048,108]{1,0:T(8,128)(2,1)S(1)} custom-call(s32[2,18]{1,0:T(2,128)S(1)} %pad_add_fusion.delays, bf16[1728,128]{1,0:T(8,128)(2,1)S(1)} %bitcast.23, bf16[1152,128]{1,0:T(8,128)(2,1)S(1)} %bitcast.26, bf16[1152,128]{1,0:T(8,128)(2,1)S(1)} %bitcast.25, f32[16,256]{1,0:T(8,128)S(1)} %convert_multiply_fusion.taps, ...), custom_call_target="tpu_custom_call" | custom-call | tf_op jit(solution)/shard_map/filterbank/pallas_call | solution.py:180
  15.1 0.0 copy-start.3
  15.1 35.2 %all_to_all.10 = bf16[256,8,108]{2,1,0:T(8,128)(2,1)S(1)} all-to-all(bf16[256,8,108]{2,1,0:T(8,128)(2,1)S(1)} %bitcast.24), channel_id=1, replica_groups={{160,162,96,98,344,346,204,206,32,34,432,434,508,510,384,386,292,294,28..., dimensions={0} | all-to-all | bytes 884736 | tf_op jit(solution)/shard_map/all_to_all | solution.py:234
  50.2 5.9 %all_gather.3.got = bf16[4096,108]{1,0:T(8,128)(2,1)S(1)} all-gather(bf16[2048,108]{1,0:T(8,128)(2,1)S(1)} %bitcast.28), channel_id=1, replica_groups=mesh['inp'=32,'y'=8,'core'=2] {'core'}, dimensions={0}, use_global_device_ids=true | all-gather | bytes 1327104 | tf_op jit(solution)/shard_map/all_gather | solution.py:236
  56.1 0.0 copy-done.3
  56.1 3.7 %correlate.1 = bf16[8,324,128]{2,1,0:T(8,128)(2,1)S(1)} custom-call(s32[1]{0:T(128)} %bitcast.2.half, s32[128]{0:T(128)S(1)} %copy-done.3, bf16[4096,108]{1,0:T(8,128)(2,1)S(1)} %all_gather.3.got), custom_call_target="tpu_custom_call" | custom-call | tf_op jit(solution)/shard_map/correlate/pallas_call | solution.py:202
  59.8 22.1 %all_to_all.11 = bf16[8,324,128]{2,1,0:T(8,128)(2,1)S(1)} all-to-all(bf16[8,324,128]{2,1,0:T(8,128)(2,1)S(1)} %correlate.1), channel_id=1, replica_groups={{0,6,12,2,8,14,4,10},{1,7,13,3,9,15,5,11},{16,22,28,18,24,30,20,26},{17..., dimensions={0} | all-to-all | bytes 1327104 | tf_op jit(solution)/shard_map/all_to_all | solution.py:238
  82.0 0.1 copy.15
  82.1 1.1 %copy.18 = f32[8,36,9,128]{3,0,2,1:T(8,128)} copy(f32[8,36,9,128]{3,0,1,2:T(8,128)S(1)} %bitcast.27) | data formatting | bytes 2654208 | tf_op jit(solution)/shard_map/reshape | solution.py:224
  (9 shorter events, 0.1 us)
Async XLA Ops:
  0.0 11.7 %copy-start.1 = (bf16[512,256]{1,0:T(8,128)(2,1)S(1)}, bf16[512,256]{1,0:T(8,128)(2,1)}, u32[]{:S(2)}) copy-start(bf16[512,256]{1,0:T(8,128)(2,1)} %constant.42.clone.low) | copy-start | bytes 786436
  0.0 11.7 %copy-start.2 = (bf16[512,256]{1,0:T(8,128)(2,1)S(1)}, bf16[512,256]{1,0:T(8,128)(2,1)}, u32[]{:S(2)}) copy-start(bf16[512,256]{1,0:T(8,128)(2,1)} %constant.41.clone.high) | copy-start | bytes 786436
  0.0 11.7 %copy-start = (bf16[18,2,6144]{2,1,0:T(2,128)(2,1)S(1)}, bf16[18,2,6144]{2,1,0:T(2,128)(2,1)}, u32[]{:S(2)}) copy-start(bf16[18,2,6144]{2,1,0:T(2,128)(2,1)} %param.6) | copy-start | bytes 1327108
  1.2 8.2 %collective-permute-start.1 = (bf16[18,64,128]{2,1,0:T(8,128)(2,1)S(1)}, bf16[18,64,128]{2,1,0:T(8,128)(2,1)S(1)}, u32[]{:S(2)}, u32[]{:S(2)}) collective-permute-start(bf16[18,64,128]{2,1,0:T(8,128)(2,1)S(1)} %get-tuple-element.11), channel_id=1, source_target_pairs={{0,15},{1,0},{2,1},{3,2},{4,3},{5,4},{6,5},{7,6},{8,7},{9,8},{10,9... | collective-permute-start | bytes 884744 | tf_op jit(solution)/shard_map/ppermute | solution.py:172
  8.0 3.7 %collective-permute-start = (bf16[18,64,128]{2,1,0:T(8,128)(2,1)S(1)}, bf16[18,64,128]{2,1,0:T(8,128)(2,1)S(1)}, u32[]{:S(2)}, u32[]{:S(2)}) collective-permute-start(bf16[18,64,128]{2,1,0:T(8,128)(2,1)S(1)} %get-tuple-element.12), channel_id=1, source_target_pairs={{0,1},{1,2},{2,3},{3,4},{4,5},{5,6},{6,7},{7,8},{8,9},{9,10},{10,1... | collective-permute-start | bytes 884744 | tf_op jit(solution)/shard_map/ppermute | solution.py:171
  15.1 41.1 %copy-start.3 = (s32[128]{0:T(128)S(1)}, s32[128]{0:T(128)}, u32[]{:S(2)}) copy-start(s32[128]{0:T(128)} %constant.40.clone.pair_at) | copy-start | bytes 1540

commit v4 on v3

--- a/solution.py
+++ b/solution.py
@@ -20,15 +20,16 @@
 
 
 def exchange_order():
-    pairs = [(p, y) for p in range(32) for y in range(0, 8, 2)]
-    shuffled = [pairs[i] for i in np.random.RandomState(0).permutation(128)]
-    return [(p, y + e) for p, y in shuffled for e in range(2)]
+    rng = np.random.RandomState(0)
+    even = [(p, y) for p in range(32) for y in range(0, 8, 2)]
+    odd = [(p, y + 1) for p, y in even]
+    even = [even[i] for i in rng.permutation(128)]
+    odd = [odd[i] for i in rng.permutation(128)]
+    return [chip for both in zip(even, odd) for chip in both]
 
 
 ORDER = exchange_order()
 GROUP = [[8 * p + y for p, y in ORDER]]
-PAIR_AT = np.asarray([ORDER.index((p, 2 * j)) // 2 for j in range(4) for p in range(32)], np.int32)
-ROWS_TO = [0, 3, 6, 1, 4, 7, 2, 5]
 
 
 def split_bf16(value):
@@ -89,8 +90,8 @@
 
     lax.fori_loop(0, SEG // AT_ONCE, some, 0)
     contract = (((1,), (1,)), ((), ()))
-    for k in range(4):
-        rows = pl.ds(LANES * k, LANES)
+    for wide in range(2):
+        rows = pl.ds(2 * LANES * wide, 2 * LANES)
         for parity in range(2):
             values = jnp.concatenate([filt[2 * parity, rows, :], filt[2 * parity + 1, rows, :]], axis=1)
             vh, vl = split_bf16(values)
@@ -100,14 +101,17 @@
             result += lax.dot_general(th, vl, contract, preferred_element_type=F32)
             result += lax.dot_general(tl, vh, contract, preferred_element_type=F32)
             for part in range(2):
-                start = parity * 8 + part * 4 + k
-                spec[pl.ds(start, 128, stride=16), :] = result[128 * part : 128 * part + 128]
+                for side in range(2):
+                    start = parity * 8 + part * 4 + 2 * wide + side
+                    spec[pl.ds(start, 128, stride=16), :] = result[
+                        128 * part : 128 * part + 128, LANES * side : LANES * side + LANES
+                    ]
     for piece in range(16):
         rows = pl.ds(128 * piece, 128)
         out[rows, :] = spec[rows, :].astype(BF16)[:, :108]
 
 
-def correlate(half, pair_at, got, out, rows_v, rows_l):
+def correlate(half, got, out, ranked, rows_v, rows_l):
     lane = lax.broadcasted_iota(jnp.int32, (16, LANES), 1)
     sign = jnp.where(lax.broadcasted_iota(jnp.int32, (8, LANES), 0) < 4, 1.0, -1.0)
     mine = half[0]
@@ -134,13 +138,19 @@
                 rows = pl.ds(pl.multiple_of((group * PER_ROW + s) * 16, 16), 16)
                 dst[rows, tile * LANES : tile * LANES + LANES] = tiles[tile].astype(BF16)
 
+    def pad(piece):
+        return jnp.concatenate([piece, jnp.zeros((16, LANES - 108), BF16)], axis=1)
+
+    for core in range(2):
+        for pair in range(128):
+            places = [core * 256 + ORDER.index((pair // 4, 2 * (pair % 4) + e)) for e in range(2)]
+            both = jnp.concatenate([got[pl.ds(8 * place, 8), :] for place in places], axis=0)
+            ranked[pl.ds(core * 2048 + 16 * pair, 16), :] = pad(both)
+
     def piece_at(group, p):
         core, pair = group // 4, group % 4
-        start = pl.multiple_of(core * 2048 + pair_at[pair * 32 + p] * 16, 16)
-        return pad(got[pl.ds(start, 16), :])
-
-    def pad(piece):
-        return jnp.concatenate([piece, jnp.zeros((16, LANES - 108), BF16)], axis=1)
+        start = pl.multiple_of(core * 2048 + p * 64 + pair * 16, 16)
+        return ranked[pl.ds(start, 16), :]
 
     def swapped(piece):
         value = piece.astype(F32)
@@ -155,12 +165,12 @@
 
     lax.fori_loop(0, 8, one, 0)
     gram = lax.dot_general(
-        rows_l[...], rows_v[...], (((0,), (0,)), ((), ())), preferred_element_type=F32
+        rows_l[:, :576], rows_v[...], (((0,), (0,)), ((), ())), preferred_element_type=F32
     ) * (1.0 / 384.0)
     both = jnp.concatenate([gram[:288, :576], gram[288:576, :576]], axis=1)
-    for place, block in enumerate(ROWS_TO):
+    for block in range(8):
         for tile in range(9):
-            out[place, pl.ds(36 * tile, 36), :] = both[
+            out[block, pl.ds(36 * tile, 36), :] = both[
                 36 * block : 36 * block + 36, LANES * tile : LANES * tile + LANES
             ].astype(BF16)
 
@@ -196,22 +206,23 @@
     )(delays, own, prev, nxt, taps, jnp.asarray(high), jnp.asarray(low))
 
 
-def run_correlate(half, pair_at, got, interpret=False):
+def run_correlate(half, got, interpret=False):
     smem = pl.BlockSpec(memory_space=pltpu.SMEM)
     vmem = pl.BlockSpec(memory_space=pltpu.VMEM)
     return pl.pallas_call(
         correlate,
         out_shape=jax.ShapeDtypeStruct((8, 324, LANES), BF16),
-        in_specs=[smem, smem, vmem],
+        in_specs=[smem, vmem],
         out_specs=vmem,
         scratch_shapes=[
+            pltpu.VMEM((4096, LANES), BF16),
             pltpu.VMEM((768, 640), BF16),
             pltpu.VMEM((768, 640), BF16),
         ],
         compiler_params=pltpu.CompilerParams(vmem_limit_bytes=48 << 20),
         interpret=interpret,
         name="correlate",
-    )(half, pair_at, got)
+    )(half, got)
 
 
 def row_major(value):
@@ -219,7 +230,6 @@
 
 
 def finish(rows):
-    rows = jnp.stack([rows[ROWS_TO.index(channel)] for channel in range(8)])
     value = rows.reshape(8, 9, 36, LANES).astype(F32)
     return value.transpose(0, 2, 1, 3).reshape(8, 36, 1152)
 
@@ -228,14 +238,14 @@
     own, prev, nxt = with_neighbours(samples)
     half = lax.axis_index("core").astype(jnp.int32).reshape(1)
     split = jnp.stack([delays // LANES, delays % LANES])
-    split, half, pair_at = lax.optimization_barrier((split, half, jnp.asarray(PAIR_AT)))
+    split, half = lax.optimization_barrier((split, half))
     coefficient = taps.astype(F32) * (1.0 / 4096.0)
     spectra = run_filterbank(split, own, prev, nxt, coefficient)
     turned = lax.all_to_all(spectra.reshape(256, 8, 108), ("inp", "y"), 0, 0, axis_index_groups=GROUP, tiled=True)
     turned = row_major(turned.reshape(2048, 108))
     both = row_major(lax.all_gather(turned, "core", axis=0, tiled=True))
-    rows = run_correlate(half, pair_at, both)
-    mine = lax.all_to_all(rows, "y", 0, 0, axis_index_groups=[ROWS_TO], tiled=True)
+    rows = run_correlate(half, both)
+    mine = lax.all_to_all(rows, "y", 0, 0, tiled=True)
     return finish(mine)
 
 

time: 84.5 us -> 84.6 us (level); the launches traced: 83.3 us -> 84.3 us
  blocking collectives: 63.1 us -> 65.1 us
    all_to_all x1, blocking collectives: 22.1 us -> 23.5 us  [shards(): mine = lax.all_to_all(rows, 'y', 0, 0, tiled=True)]
where the time goes in v4:
time: 84.6 us; the launch traced here: 84.3 us
  blocking collectives  65.1 us (77%)
  starting transfers between devices  6.85 us (8%)
  Pallas kernels  6.18 us (7%)
  local copies, waits for them, and re-layouts  2.43 us (3%)
  waiting for transfers between devices  2.27 us (3%)
  other arithmetic  1.4 us (2%)
    all_to_all x1, blocking collectives, shards(): lax.all_to_all(spectra.reshape(256, 8, 108), ('inp', 'y'), 0, 0, axis_ind...  35.6 us
    all_to_all x1, blocking collectives, shards(): mine = lax.all_to_all(rows, 'y', 0, 0, tiled=True)  23.5 us
    ppermute x1, starting transfers between devices, with_neighbours(): nxt = lax.ppermute(chunks[:, :64], ('y', 'core'), ring(-1))  6.84 us
    all_gather x1, blocking collectives, shards(): both = row_major(lax.all_gather(turned, 'core', axis=0, tiled=True))  6.06 us
    pallas_call x1, Pallas kernels, run_correlate(): pl.pallas_call(correlate, out_shape=jax.ShapeDtypeStruct((8, 324, LANES),...  3.1 us
    pallas_call x1, Pallas kernels, run_filterbank(): pl.pallas_call(filterbank, out_shape=jax.ShapeDtypeStruct((2048, 108), BF...  3.07 us
    ppermute x1, waiting for transfers between devices, with_neighbours(): prev = lax.ppermute(chunks[:, 32:], ('y', 'core'), ring(1))  2.27 us
  transfers between devices with their start and end apart: 2, of which 1 were waited for; matrix products, arithmetic and copies ran while one was open for 2% of the time, Pallas kernels for 0%

profile of v4, /device:TPU:1, one launch (start us, length us, event | category | flops | bytes accessed | tf_op | source)
XLA Modules:
  0.0 84.3 jit_solution(10347211650812518581)
XLA Ops:
  0.0 0.0 copy-start.1
  0.0 0.0 copy-start.2
  0.0 0.0 copy-start
  0.0 1.2 %fusion.2 = (bf16[18,64,128]{2,1,0:T(8,128)(2,1)S(1)}, bf16[18,64,128]{2,1,0:T(8,128)(2,1)S(1)}) fusion(bf16[18,96,128]{2,1,0:T(8,128)(2,1)} %bitcast.22), kind=kLoop, calls=%fused_computation.10 | loop fusion | bytes 1179648 | tf_op jit(solution)/shard_map/slice | solution.py:182
  1.2 6.8 %collective-permute-start.1 = (bf16[18,64,128]{2,1,0:T(8,128)(2,1)S(1)}, bf16[18,64,128]{2,1,0:T(8,128)(2,1)S(1)}, u32[]{:S(2)}, u32[]{:S(2)}) collective-permute-start(bf16[18,64,128]{2,1,0:T(8,128)(2,1)S(1)} %get-tuple-element.9), channel_id=1, source_target_pairs={{0,15},{1,0},{2,1},{3,2},{4,3},{5,4},{6,5},{7,6},{8,7},{9,8},{10,9... | collective-permute-start | bytes 884744 | tf_op jit(solution)/shard_map/ppermute | solution.py:182
  8.0 0.0 collective-permute-start
  8.0 0.7 fusion.1
  8.7 0.7 convert_multiply_fusion.taps
  9.4 0.0 collective-permute-done.1
  9.4 2.3 %collective-permute-done = bf16[18,64,128]{2,1,0:T(8,128)(2,1)S(1)} collective-permute-done((bf16[18,64,128]{2,1,0:T(8,128)(2,1)S(1)}, bf16[18,64,128]{2,1,0:T(8,128)(2,1)S(1)}, u32[]{:S(2)}, u32[]{:S(2)}) %collective-permute-start) | collective-permute-done | bytes 294944 | tf_op jit(solution)/shard_map/ppermute | solution.py:181
  11.7 0.0 copy-done.1
  11.7 0.0 copy-done.2
  11.7 0.0 copy-done
  11.7 3.1 %filterbank.1 = bf16[2048,108]{1,0:T(8,128)(2,1)S(1)} custom-call(s32[2,18]{1,0:T(2,128)S(1)} %pad_add_fusion.delays, bf16[1728,128]{1,0:T(8,128)(2,1)S(1)} %bitcast.23, bf16[1152,128]{1,0:T(8,128)(2,1)S(1)} %bitcast.26, bf16[1152,128]{1,0:T(8,128)(2,1)S(1)} %bitcast.25, f32[16,256]{1,0:T(8,128)S(1)} %convert_multiply_fusion.taps, ...), custom_call_target="tpu_custom_call" | custom-call | tf_op jit(solution)/shard_map/filterbank/pallas_call | solution.py:190
  14.8 35.6 %all_to_all.10 = bf16[256,8,108]{2,1,0:T(8,128)(2,1)S(1)} all-to-all(bf16[256,8,108]{2,1,0:T(8,128)(2,1)S(1)} %bitcast.24), channel_id=1, replica_groups={{160,358,96,434,344,298,204,438,32,286,432,506,508,418,384,194,292,402,..., dimensions={0} | all-to-all | bytes 884736 | tf_op jit(solution)/shard_map/all_to_all | solution.py:244
  50.4 6.1 %all_gather.3.got = bf16[4096,108]{1,0:T(8,128)(2,1)S(1)} all-gather(bf16[2048,108]{1,0:T(8,128)(2,1)S(1)} %bitcast.28), channel_id=1, replica_groups=mesh['inp'=32,'y'=8,'core'=2] {'core'}, dimensions={0}, use_global_device_ids=true | all-gather | bytes 1327104 | tf_op jit(solution)/shard_map/all_gather | solution.py:246
  56.4 3.1 %correlate.1 = bf16[8,324,128]{2,1,0:T(8,128)(2,1)S(1)} custom-call(s32[1]{0:T(128)} %bitcast.2.half, bf16[4096,108]{1,0:T(8,128)(2,1)S(1)} %all_gather.3.got), custom_call_target="tpu_custom_call" | custom-call | tf_op jit(solution)/shard_map/correlate/pallas_call | solution.py:212
  59.6 23.5 %all_to_all.11 = bf16[8,324,128]{2,1,0:T(8,128)(2,1)S(1)} all-to-all(bf16[8,324,128]{2,1,0:T(8,128)(2,1)S(1)} %correlate.1), channel_id=1, replica_groups=mesh['inp'=32,'y'=8,'core'=2] {'y'}, dimensions={0} | all-to-all | bytes 1327104 | tf_op jit(solution)/shard_map/all_to_all | solution.py:248
  83.1 0.1 copy.14
  83.1 1.1 %copy.17 = f32[8,36,9,128]{3,0,2,1:T(8,128)} copy(f32[8,36,9,128]{3,0,1,2:T(8,128)S(1)} %bitcast.27) | data formatting | bytes 2654208 | tf_op jit(solution)/shard_map/reshape | solution.py:234
  (1 shorter events, 0.0 us)
Async XLA Ops:
  0.0 11.7 %copy-start.1 = (bf16[512,256]{1,0:T(8,128)(2,1)S(1)}, bf16[512,256]{1,0:T(8,128)(2,1)}, u32[]{:S(2)}) copy-start(bf16[512,256]{1,0:T(8,128)(2,1)} %constant.39.clone.low) | copy-start | bytes 786436
  0.0 11.7 %copy-start.2 = (bf16[512,256]{1,0:T(8,128)(2,1)S(1)}, bf16[512,256]{1,0:T(8,128)(2,1)}, u32[]{:S(2)}) copy-start(bf16[512,256]{1,0:T(8,128)(2,1)} %constant.38.clone.high) | copy-start | bytes 786436
  0.0 11.7 %copy-start = (bf16[18,2,6144]{2,1,0:T(2,128)(2,1)S(1)}, bf16[18,2,6144]{2,1,0:T(2,128)(2,1)}, u32[]{:S(2)}) copy-start(bf16[18,2,6144]{2,1,0:T(2,128)(2,1)} %param.5) | copy-start | bytes 1327108
  1.2 8.2 %collective-permute-start.1 = (bf16[18,64,128]{2,1,0:T(8,128)(2,1)S(1)}, bf16[18,64,128]{2,1,0:T(8,128)(2,1)S(1)}, u32[]{:S(2)}, u32[]{:S(2)}) collective-permute-start(bf16[18,64,128]{2,1,0:T(8,128)(2,1)S(1)} %get-tuple-element.9), channel_id=1, source_target_pairs={{0,15},{1,0},{2,1},{3,2},{4,3},{5,4},{6,5},{7,6},{8,7},{9,8},{10,9... | collective-permute-start | bytes 884744 | tf_op jit(solution)/shard_map/ppermute | solution.py:182
  8.0 3.7 %collective-permute-start = (bf16[18,64,128]{2,1,0:T(8,128)(2,1)S(1)}, bf16[18,64,128]{2,1,0:T(8,128)(2,1)S(1)}, u32[]{:S(2)}, u32[]{:S(2)}) collective-permute-start(bf16[18,64,128]{2,1,0:T(8,128)(2,1)S(1)} %get-tuple-element.10), channel_id=1, source_target_pairs={{0,1},{1,2},{2,3},{3,4},{4,5},{5,6},{6,7},{7,8},{8,9},{9,10},{10,1... | collective-permute-start | bytes 884744 | tf_op jit(solution)/shard_map/ppermute | solution.py:181

commit v5 on v4

--- a/solution.py
+++ b/solution.py
@@ -20,7 +20,7 @@
 
 
 def exchange_order():
-    rng = np.random.RandomState(0)
+    rng = np.random.RandomState(1)
     even = [(p, y) for p in range(32) for y in range(0, 8, 2)]
     odd = [(p, y + 1) for p, y in even]
     even = [even[i] for i in rng.permutation(128)]

time: 84.6 us -> 80.8 us (0.955)
  blocking collectives: 65.1 us -> 60.9 us
    all_to_all x1, blocking collectives: 35.6 us -> 33.8 us  [shards(): lax.all_to_all(spectra.reshape(256, 8, 108), ('inp', 'y'), 0, 0, axis_ind...]
    all_gather x1, blocking collectives: 6.06 us -> 4.77 us  [shards(): both = row_major(lax.all_gather(turned, 'core', axis=0, tiled=True))]
    all_to_all x1, blocking collectives: 23.5 us -> 22.3 us  [shards(): mine = lax.all_to_all(rows, 'y', 0, 0, tiled=True)]
where the time goes in v5:
time: 80.8 us; the launch traced here: 80.1 us
  blocking collectives  60.9 us (75%)
  starting transfers between devices  6.85 us (8%)
  Pallas kernels  6.17 us (8%)
  local copies, waits for them, and re-layouts  2.43 us (3%)
  waiting for transfers between devices  2.27 us (3%)
  other arithmetic  1.4 us (2%)
    all_to_all x1, blocking collectives, shards(): lax.all_to_all(spectra.reshape(256, 8, 108), ('inp', 'y'), 0, 0, axis_ind...  33.8 us
    all_to_all x1, blocking collectives, shards(): mine = lax.all_to_all(rows, 'y', 0, 0, tiled=True)  22.3 us
    ppermute x1, starting transfers between devices, with_neighbours(): nxt = lax.ppermute(chunks[:, :64], ('y', 'core'), ring(-1))  6.84 us
    all_gather x1, blocking collectives, shards(): both = row_major(lax.all_gather(turned, 'core', axis=0, tiled=True))  4.77 us
    pallas_call x1, Pallas kernels, run_correlate(): pl.pallas_call(correlate, out_shape=jax.ShapeDtypeStruct((8, 324, LANES),...  3.1 us
    pallas_call x1, Pallas kernels, run_filterbank(): pl.pallas_call(filterbank, out_shape=jax.ShapeDtypeStruct((2048, 108), BF...  3.06 us
    ppermute x1, waiting for transfers between devices, with_neighbours(): prev = lax.ppermute(chunks[:, 32:], ('y', 'core'), ring(1))  2.27 us
  transfers between devices with their start and end apart: 2, of which 1 were waited for; matrix products, arithmetic and copies ran while one was open for 2% of the time, Pallas kernels for 0%

profile of v5, /device:TPU:1, one launch (start us, length us, event | category | flops | bytes accessed | tf_op | source)
XLA Modules:
  0.0 80.1 jit_solution(7754158321994662337)
XLA Ops:
  0.0 0.0 copy-start.1
  0.0 0.0 copy-start.2
  0.0 0.0 copy-start
  0.0 1.2 %fusion.2 = (bf16[18,64,128]{2,1,0:T(8,128)(2,1)S(1)}, bf16[18,64,128]{2,1,0:T(8,128)(2,1)S(1)}) fusion(bf16[18,96,128]{2,1,0:T(8,128)(2,1)} %bitcast.22), kind=kLoop, calls=%fused_computation.10 | loop fusion | bytes 1179648 | tf_op jit(solution)/shard_map/slice | solution.py:182
  1.2 6.8 %collective-permute-start.1 = (bf16[18,64,128]{2,1,0:T(8,128)(2,1)S(1)}, bf16[18,64,128]{2,1,0:T(8,128)(2,1)S(1)}, u32[]{:S(2)}, u32[]{:S(2)}) collective-permute-start(bf16[18,64,128]{2,1,0:T(8,128)(2,1)S(1)} %get-tuple-element.9), channel_id=1, source_target_pairs={{0,15},{1,0},{2,1},{3,2},{4,3},{5,4},{6,5},{7,6},{8,7},{9,8},{10,9... | collective-permute-start | bytes 884744 | tf_op jit(solution)/shard_map/ppermute | solution.py:182
  8.0 0.0 collective-permute-start
  8.0 0.7 fusion.1
  8.7 0.7 convert_multiply_fusion.taps
  9.4 0.0 collective-permute-done.1
  9.4 2.3 %collective-permute-done = bf16[18,64,128]{2,1,0:T(8,128)(2,1)S(1)} collective-permute-done((bf16[18,64,128]{2,1,0:T(8,128)(2,1)S(1)}, bf16[18,64,128]{2,1,0:T(8,128)(2,1)S(1)}, u32[]{:S(2)}, u32[]{:S(2)}) %collective-permute-start) | collective-permute-done | bytes 294944 | tf_op jit(solution)/shard_map/ppermute | solution.py:181
  11.7 0.0 copy-done.1
  11.7 0.0 copy-done.2
  11.7 0.0 copy-done
  11.7 3.1 %filterbank.1 = bf16[2048,108]{1,0:T(8,128)(2,1)S(1)} custom-call(s32[2,18]{1,0:T(2,128)S(1)} %pad_add_fusion.delays, bf16[1728,128]{1,0:T(8,128)(2,1)S(1)} %bitcast.23, bf16[1152,128]{1,0:T(8,128)(2,1)S(1)} %bitcast.26, bf16[1152,128]{1,0:T(8,128)(2,1)S(1)} %bitcast.25, f32[16,256]{1,0:T(8,128)S(1)} %convert_multiply_fusion.taps, ...), custom_call_target="tpu_custom_call" | custom-call | tf_op jit(solution)/shard_map/filterbank/pallas_call | solution.py:190
  14.8 33.8 %all_to_all.10 = bf16[256,8,108]{2,1,0:T(8,128)(2,1)S(1)} all-to-all(bf16[256,8,108]{2,1,0:T(8,128)(2,1)S(1)} %bitcast.24), channel_id=1, replica_groups={{484,6,416,230,220,354,224,382,132,274,472,18,488,374,140,110,124,506,2..., dimensions={0} | all-to-all | bytes 884736 | tf_op jit(solution)/shard_map/all_to_all | solution.py:244
  48.6 4.8 %all_gather.3.got = bf16[4096,108]{1,0:T(8,128)(2,1)S(1)} all-gather(bf16[2048,108]{1,0:T(8,128)(2,1)S(1)} %bitcast.28), channel_id=1, replica_groups=mesh['inp'=32,'y'=8,'core'=2] {'core'}, dimensions={0}, use_global_device_ids=true | all-gather | bytes 1327104 | tf_op jit(solution)/shard_map/all_gather | solution.py:246
  53.4 3.1 %correlate.1 = bf16[8,324,128]{2,1,0:T(8,128)(2,1)S(1)} custom-call(s32[1]{0:T(128)} %bitcast.2.half, bf16[4096,108]{1,0:T(8,128)(2,1)S(1)} %all_gather.3.got), custom_call_target="tpu_custom_call" | custom-call | tf_op jit(solution)/shard_map/correlate/pallas_call | solution.py:212
  56.5 22.3 %all_to_all.11 = bf16[8,324,128]{2,1,0:T(8,128)(2,1)S(1)} all-to-all(bf16[8,324,128]{2,1,0:T(8,128)(2,1)S(1)} %correlate.1), channel_id=1, replica_groups=mesh['inp'=32,'y'=8,'core'=2] {'y'}, dimensions={0} | all-to-all | bytes 1327104 | tf_op jit(solution)/shard_map/all_to_all | solution.py:248
  78.8 0.1 copy.14
  78.9 1.1 %copy.17 = f32[8,36,9,128]{3,0,2,1:T(8,128)} copy(f32[8,36,9,128]{3,0,1,2:T(8,128)S(1)} %bitcast.27) | data formatting | bytes 2654208 | tf_op jit(solution)/shard_map/reshape | solution.py:234
  (1 shorter events, 0.0 us)
Async XLA Ops:
  0.0 11.7 %copy-start.1 = (bf16[512,256]{1,0:T(8,128)(2,1)S(1)}, bf16[512,256]{1,0:T(8,128)(2,1)}, u32[]{:S(2)}) copy-start(bf16[512,256]{1,0:T(8,128)(2,1)} %constant.39.clone.low) | copy-start | bytes 786436
  0.0 11.7 %copy-start.2 = (bf16[512,256]{1,0:T(8,128)(2,1)S(1)}, bf16[512,256]{1,0:T(8,128)(2,1)}, u32[]{:S(2)}) copy-start(bf16[512,256]{1,0:T(8,128)(2,1)} %constant.38.clone.high) | copy-start | bytes 786436
  0.0 11.7 %copy-start = (bf16[18,2,6144]{2,1,0:T(2,128)(2,1)S(1)}, bf16[18,2,6144]{2,1,0:T(2,128)(2,1)}, u32[]{:S(2)}) copy-start(bf16[18,2,6144]{2,1,0:T(2,128)(2,1)} %param.5) | copy-start | bytes 1327108
  1.2 8.2 %collective-permute-start.1 = (bf16[18,64,128]{2,1,0:T(8,128)(2,1)S(1)}, bf16[18,64,128]{2,1,0:T(8,128)(2,1)S(1)}, u32[]{:S(2)}, u32[]{:S(2)}) collective-permute-start(bf16[18,64,128]{2,1,0:T(8,128)(2,1)S(1)} %get-tuple-element.9), channel_id=1, source_target_pairs={{0,15},{1,0},{2,1},{3,2},{4,3},{5,4},{6,5},{7,6},{8,7},{9,8},{10,9... | collective-permute-start | bytes 884744 | tf_op jit(solution)/shard_map/ppermute | solution.py:182
  8.0 3.7 %collective-permute-start = (bf16[18,64,128]{2,1,0:T(8,128)(2,1)S(1)}, bf16[18,64,128]{2,1,0:T(8,128)(2,1)S(1)}, u32[]{:S(2)}, u32[]{:S(2)}) collective-permute-start(bf16[18,64,128]{2,1,0:T(8,128)(2,1)S(1)} %get-tuple-element.10), channel_id=1, source_target_pairs={{0,1},{1,2},{2,3},{3,4},{4,5},{5,6},{6,7},{7,8},{8,9},{9,10},{10,1... | collective-permute-start | bytes 884744 | tf_op jit(solution)/shard_map/ppermute | solution.py:181
